TPU v7x, 256 devices: a whole 4x4x8 slice. The times are simulated.
256 devices in a mesh: edge: 64 (over y, z, x_lo), chan: 4 (over x_hi, core).
Axes of the slice: x: 4 (x_hi: 2, x_lo: 2; x = x_hi * 2 + x_lo), y: 4, z: 8, core: 2. Of those that a mesh axis runs over, the one named last changes fastest.
Arguments:
- node_states: bfloat16 [1024, 49, 256], P('edge', None, 'chan'), may hold values from -6 to 6
- edge_vectors: float32 [3, 32768], P(None, ('edge', 'chan')), may hold values from -5.6 to 5.6, as said below
- source_part: int32 [32768, 1], P('edge'), may hold values from 0 to 63; in each aligned block of 512 rows (0 to 511, 512 to 1023, ...) at most 16 rows name the same one
- source_slot: int32 [32768], P('edge'), may hold values from 0 to 15
- target_slot: int32 [32768], P('edge'), may hold values from 0 to 15
- live_edges: int32 [64], P('edge'), may hold values from 1 to 512, 24576 in all
- weight_zero: bfloat16 [7, 256, 7, 256], P(None, 'chan'), may hold values from -0.125 to 0.125
- weight_one: bfloat16 [2, 6, 256, 6, 256], P(None, None, 'chan'), may hold values from -0.109375 to 0.109375
- weight_two: bfloat16 [2, 5, 256, 5, 256], P(None, None, 'chan'), may hold values from -0.125 to 0.125
Outputs:
- aggregated: bfloat16 [1024, 49, 256], P('edge', None, 'chan')
Inputs may be any that keep to these rules, and one draw needn't show every extreme that they name: `source_part`: in each aligned block of 512 rows (the edges of one partition's slab) no partition number appears more than 16 times, and some number appears exactly 16 times. Edges are grouped by destination partition: the destination of an edge in slab p is node p * 16 + target_slot. `live_edges`: live slots stand at the front of each slab; the fullest slab is full. `edge_vectors`: every column has length between 0.8 and 5.6.
All inputs are finite; a program needn't handle non-finite values. No bound on the sum of `live_edges` on one device may be relied on, other than what follows from the above.
Results may differ from a plain program's by a relative error of at most 0.015.
Values may be sent and summed in bfloat16 or wider, within the bound.
No kernel may reach another device: no remote copies, remote signals or barrier semaphores. Data moves between devices by JAX's collectives and lax.ppermute only.
A program may use at most 128 MiB of HBM per device.

v0:
```python
import math

import jax
import jax.numpy as jnp
import numpy as np
from jax import lax
from jax.sharding import PartitionSpec as P

LMAX = 6
MMAX = 2


cutoff_radius = 6.0
highest = lax.Precision.HIGHEST


def harmonics(coord_x, coord_y, coord_z, degree_top, order_top):
    results = {}
    real_part = [coord_x * 0.0 + 1.0]
    imag_part = [coord_x * 0.0]
    for azimuthal in range(1, order_top + 1):
        new_real = coord_x * real_part[-1] - coord_y * imag_part[-1]
        new_imag = coord_x * imag_part[-1] + coord_y * real_part[-1]
        real_part.append(new_real)
        imag_part.append(new_imag)
    for azimuthal in range(order_top + 1):
        start_value = (-1.0) ** azimuthal * math.prod(range(2 * azimuthal - 1, 0, -2))
        legendre = {azimuthal: coord_z * 0.0 + start_value}
        if azimuthal + 1 <= degree_top:
            legendre[azimuthal + 1] = coord_z * ((2 * azimuthal + 1) * start_value)
        for degree in range(azimuthal + 2, degree_top + 1):
            legendre[degree] = (
                (2 * degree - 1) * coord_z * legendre[degree - 1]
                - (degree + azimuthal - 1) * legendre[degree - 2]
            ) / (degree - azimuthal)
        for degree in range(azimuthal, degree_top + 1):
            factor = math.sqrt(
                (2 * degree + 1)
                / (4.0 * math.pi)
                * math.factorial(degree - azimuthal)
                / math.factorial(degree + azimuthal)
            )
            if azimuthal == 0:
                results[degree, 0] = factor * legendre[degree]
            else:
                results[degree, azimuthal] = (
                    math.sqrt(2.0) * factor * legendre[degree] * real_part[azimuthal]
                )
                results[degree, -azimuthal] = (
                    math.sqrt(2.0) * factor * legendre[degree] * imag_part[azimuthal]
                )
    return results


def kept_rows():
    row_list = [(degree, 0) for degree in range(LMAX + 1)]
    for azimuthal in range(1, MMAX + 1):
        row_list += [(degree, azimuthal) for degree in range(azimuthal, LMAX + 1)]
        row_list += [(degree, -azimuthal) for degree in range(azimuthal, LMAX + 1)]
    return row_list


def row_offsets():
    listing = []
    offset = 0
    for degree, azimuthal in kept_rows():
        listing.append((degree, offset))
        offset += 2 * degree + 1
    return listing


def invert_small(matrix):
    order_size = matrix.shape[0]
    work = np.concatenate([matrix, np.eye(order_size)], axis=1)
    for column in range(order_size):
        work[column] = work[column] / work[column, column]
        for row_index in range(order_size):
            if row_index != column:
                work[row_index] = work[row_index] - work[row_index, column] * work[column]
    return work[:, order_size:]


def sample_tables():
    sample_count = 2 * (LMAX + 1) ** 2
    positions = np.arange(sample_count) + 0.5
    height = 1.0 - 2.0 * positions / sample_count
    radius = np.sqrt(1.0 - height * height)
    azimuth = math.pi * (3.0 - math.sqrt(5.0)) * positions
    points = np.stack([radius * np.cos(azimuth), radius * np.sin(azimuth), height])
    values = harmonics(points[0], points[1], points[2], LMAX, LMAX)
    inverses = []
    for degree in range(LMAX + 1):
        sampled = np.stack([values[degree, azimuthal] for azimuthal in range(-degree, degree + 1)])
        inverses.append(sampled.T @ invert_small(sampled @ sampled.T))
    return (points, inverses)


def wigner_rows(vectors):
    length = jnp.sqrt(jnp.sum(vectors * vectors, axis=0))
    direction = vectors / length
    pick_first = jnp.where(jnp.abs(direction[0]) < 0.6, 1.0, 0.0).astype(jnp.float32)
    helper = jnp.stack([pick_first, 1.0 - pick_first, jnp.zeros_like(pick_first)])
    first_axis = jnp.cross(direction, helper, axis=0)
    first_axis = first_axis / jnp.sqrt(jnp.sum(first_axis * first_axis, axis=0))
    second_axis = jnp.cross(direction, first_axis, axis=0)
    frames = jnp.stack([first_axis, second_axis, direction])
    points, inverses = sample_tables()
    sample = jnp.asarray(points, jnp.float32)
    turned = jnp.einsum("rce,ck->rek", frames, sample, precision=highest)
    values = harmonics(turned[0], turned[1], turned[2], LMAX, MMAX)
    pieces = []
    for degree, azimuthal in kept_rows():
        table = jnp.asarray(inverses[degree], jnp.float32)
        pieces.append(jnp.dot(values[degree, azimuthal], table, precision=highest))
    compact = jnp.concatenate(pieces, axis=1)
    envelope = 0.5 * (jnp.cos(math.pi * length / cutoff_radius) + 1.0)
    return (compact, envelope)


def rotate_forward(compact_t, sources):
    rows_out = []
    for degree, offset in row_offsets():
        total = compact_t[offset].astype(jnp.float32)[None, :] * sources[degree * degree].astype(
            jnp.float32
        )
        for inner in range(1, 2 * degree + 1):
            total = total + compact_t[offset + inner].astype(jnp.float32)[None, :] * sources[
                degree * degree + inner
            ].astype(jnp.float32)
        rows_out.append(total)
    return jnp.stack(rows_out, axis=0).astype(jnp.bfloat16)


def rotate_back(compact_t, scaled):
    listing = row_offsets()
    coefs_out = []
    for degree in range(LMAX + 1):
        for inner in range(2 * degree + 1):
            total = None
            for row_index, (row_degree, offset) in enumerate(listing):
                if row_degree == degree:
                    term = compact_t[offset + inner].astype(jnp.float32)[None, :] * scaled[
                        :, row_index
                    ].astype(jnp.float32)
                    total = term if total is None else total + term
            coefs_out.append(total)
    return jnp.stack(coefs_out, axis=0).astype(jnp.bfloat16)


def convolve(turned, weight_zero, weight_one, weight_two, contract):
    end_zero = LMAX + 1
    end_one_plus = end_zero + LMAX
    end_one_minus = end_one_plus + LMAX
    end_two_plus = end_one_minus + LMAX - 1
    zero_part = turned[:end_zero]
    one_plus = turned[end_zero:end_one_plus]
    one_minus = turned[end_one_plus:end_one_minus]
    two_plus = turned[end_one_minus:end_two_plus]
    two_minus = turned[end_two_plus:]
    pattern = "lce,lcjd->dje"
    out_zero = contract(pattern, zero_part, weight_zero)
    out_one_plus = contract(pattern, one_plus, weight_one[0]) - contract(
        pattern, one_minus, weight_one[1]
    )
    out_one_minus = contract(pattern, one_minus, weight_one[0]) + contract(
        pattern, one_plus, weight_one[1]
    )
    out_two_plus = contract(pattern, two_plus, weight_two[0]) - contract(
        pattern, two_minus, weight_two[1]
    )
    out_two_minus = contract(pattern, two_minus, weight_two[0]) + contract(
        pattern, two_plus, weight_two[1]
    )
    return jnp.concatenate(
        [out_zero, out_one_plus, out_one_minus, out_two_plus, out_two_minus], axis=1
    )


def mixed_contract(pattern, first_operand, second_operand):
    return jnp.einsum(pattern, first_operand, second_operand, preferred_element_type=jnp.float32)


def one_hot(indices, width):
    return (indices[:, None] == jnp.arange(width, dtype=jnp.int32)[None, :]).astype(jnp.bfloat16)


def pick_columns(table, selector):
    picked = lax.dot_general(
        table, selector, (((0,), (1,)), ((), ())), preferred_element_type=jnp.float32
    )
    return picked.astype(jnp.bfloat16)


def pick_rows(selector, table):
    return jnp.dot(selector, table, preferred_element_type=jnp.float32).astype(jnp.bfloat16)


def shards(
    node_states,
    edge_vectors,
    source_part,
    source_slot,
    target_slot,
    live_edges,
    weight_zero,
    weight_one,
    weight_two,
):
    slab_size = source_slot.shape[0]
    local_nodes = node_states.shape[0]
    local_channels = node_states.shape[2]
    coef_count = node_states.shape[1]
    group_count = lax.axis_size("edge")
    capacity = max(2, 2 * slab_size // group_count)
    slot_total = group_count * capacity
    quarter, quarter_fade = wigner_rows(edge_vectors)
    compact, envelope = (
        lax.all_gather(quarter.astype(jnp.bfloat16), "chan", axis=0, tiled=True),
        lax.all_gather(quarter_fade.astype(jnp.bfloat16), "chan", axis=0, tiled=True),
    )
    compact_t = compact.T
    node_flat = node_states.reshape(local_nodes, coef_count * local_channels)
    owner_part = source_part[:, 0]
    owners = jnp.arange(group_count, dtype=jnp.int32)
    member = (owner_part[:, None] == owners[None, :]).astype(jnp.int32)
    earlier = jnp.cumsum(member, axis=0) - member
    position = jnp.sum(earlier * member, axis=1)
    slot_flat = owner_part * capacity + position
    requests = (
        jnp.zeros((slot_total,), jnp.int32)
        .at[slot_flat]
        .set(source_slot)
        .reshape(group_count, capacity)
    )
    slot_select = one_hot(slot_flat, slot_total)
    wanted = lax.all_to_all(requests, "edge", split_axis=0, concat_axis=0, tiled=True)
    picked = pick_rows(one_hot(wanted.reshape(-1), local_nodes), node_flat)
    returned = lax.all_to_all(
        picked.reshape(group_count, capacity, coef_count * local_channels),
        "edge",
        split_axis=0,
        concat_axis=0,
        tiled=True,
    )
    sources = pick_columns(
        returned.reshape(slot_total, coef_count * local_channels), slot_select
    ).reshape(coef_count, local_channels, slab_size)
    turned = rotate_forward(compact_t, sources)
    channel_mix = lax.psum_scatter(
        convolve(turned, weight_zero, weight_one, weight_two, mixed_contract).astype(jnp.bfloat16),
        "chan",
        scatter_dimension=0,
        tiled=True,
    ).astype(jnp.float32)
    alive_mask = (jnp.arange(slab_size, dtype=jnp.int32) < live_edges[0]).astype(jnp.float32)
    scaling = envelope.astype(jnp.float32) * alive_mask
    scaled = (channel_mix * scaling).astype(jnp.bfloat16)
    message = rotate_back(compact_t, scaled).reshape(coef_count * local_channels, slab_size)
    selector = (jnp.arange(local_nodes, dtype=jnp.int32)[:, None] == target_slot[None, :]).astype(
        jnp.bfloat16
    )
    summed = lax.dot_general(
        selector, message, (((1,), (1,)), ((), ())), preferred_element_type=jnp.float32
    )
    return summed.astype(jnp.bfloat16).reshape(local_nodes, coef_count, local_channels)


def solution(mesh):
    in_specs = (
        P("edge", None, "chan"),
        P(None, ("edge", "chan")),
        P("edge", None),
        P("edge"),
        P("edge"),
        P("edge"),
        P(None, "chan", None, None),
        P(None, None, "chan", None, None),
        P(None, None, "chan", None, None),
    )
    out_specs = P("edge", None, "chan")
    return jax.shard_map(shards, mesh=mesh, in_specs=in_specs, out_specs=out_specs, check_vma=False)
```

profile of v0, /device:TPU:1, one launch (start us, length us, event | category | flops | bytes accessed | tf_op | source)
XLA Modules:
  0.0 345.9 jit_solution(5656310908398579439)
XLA Ops:
  6.5 0.8 fusion.497
  7.4 1.2 reduce-window.6
  8.8 0.8 fusion.490
  9.6 1.3 compare_select_fusion
  10.9 2.6 scatter_custom_fusion
  13.5 0.7 all_to_all.9
  14.2 13.6 %all-to-all-start = ((s32[64,1,16]{2,1,0:T(1,128)}), s32[64,1,16]{2,1,0:T(1,128)S(1)}, u32[]{:S(2)}, u32[]{:S(2)}) async-start(s32[64,1,16]{2,1,0:T(1,128)} %bitcast.27), calls=%async_computation | async-start | bytes 65536 | tf_op jit(solution)/shard_map/all_to_all | solution.py:236
  27.8 0.7 multiply_reduce_fusion.1
  28.5 1.0 copy.58
  29.7 7.3 %all-to-all-done = s32[64,1,16]{2,1,0:T(1,128)S(1)} async-done(((s32[64,1,16]{2,1,0:T(1,128)}), s32[64,1,16]{2,1,0:T(1,128)S(1)}, u32[]{:S(2)}, u32[]{:S(2)}) %all-to-all-start) | async-done | bytes 4128 | tf_op jit(solution)/shard_map/all_to_all | solution.py:236
  36.9 0.5 broadcast.6397
  37.5 0.7 reduce.5
  38.3 4.7 %convolution_convert_fusion = bf16[1024,3136]{0,1:T(8,128)(2,1)} fusion(bf16[16,3136]{1,0:T(8,128)(2,1)S(1)} %reshape.10748, s32[1024]{0:T(1024)S(1)} %eq.79), kind=kOutput, calls=%fused_computation.1 | convolution fusion | flops 105988096 | bytes 6526976 | tf_op jit(solution)/shard_map/dot_general | solution.py:195
  42.9 9.3 %copy.59 = bf16[1024,3136]{1,0:T(8,128)(2,1)} copy(bf16[1024,3136]{0,1:T(8,128)(2,1)} %convolution_convert_fusion) | data formatting | bytes 12845056 | tf_op jit(solution)/shard_map/convert_element_type | solution.py:195
  52.3 5.8 %all-to-all-start.1 = ((bf16[64,16,3136]{2,1,0:T(8,128)(2,1)}), bf16[64,16,3136]{2,1,0:T(8,128)(2,1)}, u32[]{:S(2)}, u32[]{:S(2)}) async-start(bf16[64,16,3136]{2,1,0:T(8,128)(2,1)} %bitcast.1286), calls=%async_computation.1 | async-start | bytes 13107200 | tf_op jit(solution)/shard_map/all_to_all | solution.py:238
  58.2 0.6 convert_bitcast_fusion
  59.0 0.4 fusion.657
  60.2 0.2 convolution_convert_fusion.17
  62.7 0.2 convolution_convert_fusion.20
  63.7 0.2 convolution_convert_fusion.13
  64.2 0.2 convolution_convert_fusion.11
  64.5 0.2 convolution_convert_fusion.10
  65.0 0.3 convolution_convert_fusion.8
  65.5 0.2 convolution_convert_fusion.6
  65.7 0.2 convolution_convert_fusion.5
  66.2 0.2 convolution_convert_fusion.3
  66.5 2.1 concatenate.16
  68.6 9.9 %all_gather.6 = bf16[512,235]{0,1:T(8,128)(2,1)S(1)} all-gather(bf16[128,235]{0,1:T(8,128)(2,1)S(1)} %concatenate.16), channel_id=1, replica_groups=mesh['edge'=64,'chan'=4] {'chan'}, dimensions={0}, use_global_device_ids=true | all-gather | bytes 300800 | tf_op jit(solution)/shard_map/all_gather | solution.py:218
  78.5 0.7 slice_convert_fusion.225
  79.1 0.6 slice_convert_fusion.77
  79.8 0.6 slice_convert_fusion.39
  80.4 0.6 slice_convert_fusion.129
  81.0 0.7 slice_convert_fusion.23
  81.7 0.7 slice_convert_fusion.209
  82.3 0.6 slice_convert_fusion.185
  83.0 0.7 slice_convert_fusion.170
  83.6 0.6 slice_convert_fusion.150
  84.3 0.7 slice_convert_fusion.113
  84.9 0.7 slice_convert_fusion.57
  85.6 0.7 slice_convert_fusion.12
  86.3 1.3 fusion.803
  87.6 1.2 fusion.802
  88.8 113.9 %all-to-all-done.1 = bf16[64,16,3136]{2,1,0:T(8,128)(2,1)} async-done(((bf16[64,16,3136]{2,1,0:T(8,128)(2,1)}), bf16[64,16,3136]{2,1,0:T(8,128)(2,1)}, u32[]{:S(2)}, u32[]{:S(2)}) %all-to-all-start.1) | async-done | bytes 6422560 | tf_op jit(solution)/shard_map/all_to_all | solution.py:238
  203.0 7.0 %convolution_convert_fusion.1 = bf16[3136,512]{1,0:T(8,128)(2,1)S(1)} fusion(bf16[1024,3136]{1,0:T(8,128)(2,1)} %bitcast.29, s32[512]{0:T(512)} %bitcast.1775), kind=kOutput, calls=%fused_computation.2 | convolution fusion | flops 3290464256 | bytes 9635840 | tf_op jit(solution)/shard_map/dot_general | solution.py:188
  210.3 0.9 constant_dynamic-update-slice_fusion.17
  211.2 0.8 constant_dynamic-update-slice_fusion.11
  212.0 0.8 constant_dynamic-update-slice_fusion.10
  213.7 1.0 fusion.12
  215.9 1.0 fusion.11
  217.5 0.8 constant_dynamic-update-slice_fusion.21
  219.0 0.9 fusion.14
  220.8 0.9 fusion.13
  222.6 2.5 bitcast_dynamic-update-slice_fusion
  225.0 2.2 bitcast_dynamic-update-slice_fusion.2
  227.3 2.2 bitcast_dynamic-update-slice_fusion.1
  229.4 2.0 fusion.5
  231.4 1.9 fusion.7
  233.4 14.5 %copy.65 = bf16[256,29,512]{2,1,0:T(8,128)(2,1)} copy(bf16[256,29,512]{0,2,1:T(8,128)(2,1)} %fusion.7) | data formatting | bytes 15204352 | tf_op jit(solution)/shard_map/concatenate | solution.py:174
  248.0 0.5 copy-done.205
  248.5 9.3 %all-gather = bf16[4,1,128]{2,1,0:T(2,128)(2,1)S(1)} all-gather(bf16[1,1,128]{2,1,0:T(2,128)(2,1)S(1)} %copy-done.205), channel_id=1, replica_groups=mesh['edge'=64,'chan'=4] {'chan'}, dimensions={0}, use_global_device_ids=true | all-gather | bytes 1280 | tf_op jit(solution)/shard_map/all_gather | solution.py:219
  258.6 71.5 %reduce-scatter.2.cloned.1.call-done = bf16[64,29,512]{2,1,0:T(8,128)(2,1)} async-done(((bf16[256,29,512]{2,1,0:T(8,128)(2,1)}), bf16[64,29,512]{2,1,0:T(8,128)(2,1)}) %reduce-scatter.2.cloned.1.call-update) | async-done | bytes 1900560 | tf_op jit(solution)/shard_map/reduce_scatter | solution.py:249
  330.1 2.7 multiply_convert_fusion
  337.2 0.9 convolution_convert_fusion.2
  338.3 0.7 copy.67
  (534 shorter events, 12.8 us)
Async XLA Ops:
  6.5 216.0 %copy-start = (bf16[7,64,7,256]{3,1,2,0:T(8,128)(2,1)S(1)}, bf16[7,64,7,256]{3,1,2,0:T(8,128)(2,1)}, u32[]{:S(2)}) copy-start(bf16[7,64,7,256]{3,1,2,0:T(8,128)(2,1)} %param.47) | copy-start | bytes 4816900
  14.2 22.7 %all-to-all-start = ((s32[64,1,16]{2,1,0:T(1,128)}), s32[64,1,16]{2,1,0:T(1,128)S(1)}, u32[]{:S(2)}, u32[]{:S(2)}) async-start(s32[64,1,16]{2,1,0:T(1,128)} %bitcast.27), calls=%async_computation | async-start | bytes 65536 | tf_op jit(solution)/shard_map/all_to_all | solution.py:236
  52.2 7.5 %copy-start.4 = (f32[98,5]{1,0:T(8,128)S(1)}, f32[98,5]{1,0:T(8,128)}, u32[]{:S(2)}) copy-start(f32[98,5]{1,0:T(8,128)} %constant.147.clone) | copy-start | bytes 5884
  52.2 7.8 %copy-start.9 = (f32[98,7]{1,0:T(8,128)S(1)}, f32[98,7]{1,0:T(8,128)}, u32[]{:S(2)}) copy-start(f32[98,7]{1,0:T(8,128)} %constant.148.clone) | copy-start | bytes 8236
  52.2 8.0 %copy-start.208 = (f32[98,9]{1,0:T(8,128)S(1)}, f32[98,9]{1,0:T(8,128)}, u32[]{:S(2)}) copy-start(f32[98,9]{1,0:T(8,128)} %constant.149.clone) | copy-start | bytes 10588
  52.2 8.2 %copy-start.207 = (f32[98,11]{1,0:T(8,128)S(1)}, f32[98,11]{1,0:T(8,128)}, u32[]{:S(2)}) copy-start(f32[98,11]{1,0:T(8,128)} %constant.150.clone) | copy-start | bytes 12940
  52.3 8.5 %copy-start.206 = (f32[98,13]{1,0:T(8,128)S(1)}, f32[98,13]{1,0:T(8,128)}, u32[]{:S(2)}) copy-start(f32[98,13]{1,0:T(8,128)} %constant.151.clone) | copy-start | bytes 15292
  52.3 150.4 %all-to-all-start.1 = ((bf16[64,16,3136]{2,1,0:T(8,128)(2,1)}), bf16[64,16,3136]{2,1,0:T(8,128)(2,1)}, u32[]{:S(2)}, u32[]{:S(2)}) async-start(bf16[64,16,3136]{2,1,0:T(8,128)(2,1)} %bitcast.1286), calls=%async_computation.1 | async-start | bytes 13107200 | tf_op jit(solution)/shard_map/all_to_all | solution.py:238
  58.1 272.0 %reduce-scatter.2.cloned.1.call-start = ((), (), s32[]{:S(2)}) async-start(), calls=%async_computation.3 | async-start | bytes 10485760 | tf_op jit(solution)/shard_map/reduce_scatter | solution.py:249
  62.2 24.0 %copy-start.3 = (bf16[2,5,64,5,256]{4,2,3,1,0:T(8,128)(2,1)S(1)}, bf16[2,5,64,5,256]{4,2,3,1,0:T(8,128)(2,1)}, u32[]{:S(2)}) copy-start(bf16[2,5,64,5,256]{4,2,3,1,0:T(8,128)(2,1)} %param.49) | copy-start | bytes 4915204
  68.5 19.0 %copy-start.2 = (bf16[2,6,64,6,256]{4,2,3,1,0:T(8,128)(2,1)S(1)}, bf16[2,6,64,6,256]{4,2,3,1,0:T(8,128)(2,1)}, u32[]{:S(2)}) copy-start(bf16[2,6,64,6,256]{4,2,3,1,0:T(8,128)(2,1)} %param.48) | copy-start | bytes 7077892
  202.7 7.4 %copy-start.112 = (f32[1,512]{1,0:T(1,128)S(1)}, f32[1,512]{1,0:T(1,128)}, u32[]{:S(2)}) copy-start(f32[1,512]{1,0:T(1,128)} %get-tuple-element.68) | copy-start | bytes 6148
  202.7 7.4 %copy-start.118 = (f32[1,512]{1,0:T(1,128)S(1)}, f32[1,512]{1,0:T(1,128)}, u32[]{:S(2)}) copy-start(f32[1,512]{1,0:T(1,128)} %get-tuple-element.69) | copy-start | bytes 6148
  202.7 7.4 %copy-start.151 = (f32[1,512]{1,0:T(1,128)S(1)}, f32[1,512]{1,0:T(1,128)}, u32[]{:S(2)}) copy-start(f32[1,512]{1,0:T(1,128)} %get-tuple-element.160) | copy-start | bytes 6148
  202.7 7.4 %copy-start.157 = (f32[1,512]{1,0:T(1,128)S(1)}, f32[1,512]{1,0:T(1,128)}, u32[]{:S(2)}) copy-start(f32[1,512]{1,0:T(1,128)} %get-tuple-element.161) | copy-start | bytes 6148
  202.7 7.4 %copy-start.163 = (f32[1,512]{1,0:T(1,128)S(1)}, f32[1,512]{1,0:T(1,128)}, u32[]{:S(2)}) copy-start(f32[1,512]{1,0:T(1,128)} %get-tuple-element.162) | copy-start | bytes 6148
  202.7 7.5 %copy-start.115 = (f32[1,512]{1,0:T(1,128)S(1)}, f32[1,512]{1,0:T(1,128)}, u32[]{:S(2)}) copy-start(f32[1,512]{1,0:T(1,128)} %get-tuple-element.155) | copy-start | bytes 6148
  202.7 7.5 %copy-start.120 = (f32[1,512]{1,0:T(1,128)S(1)}, f32[1,512]{1,0:T(1,128)}, u32[]{:S(2)}) copy-start(f32[1,512]{1,0:T(1,128)} %get-tuple-element.156) | copy-start | bytes 6148
  202.7 7.5 %copy-start.125 = (f32[1,512]{1,0:T(1,128)S(1)}, f32[1,512]{1,0:T(1,128)}, u32[]{:S(2)}) copy-start(f32[1,512]{1,0:T(1,128)} %get-tuple-element.157) | copy-start | bytes 6148
  202.7 7.5 %copy-start.133 = (f32[1,512]{1,0:T(1,128)S(1)}, f32[1,512]{1,0:T(1,128)}, u32[]{:S(2)}) copy-start(f32[1,512]{1,0:T(1,128)} %get-tuple-element.158) | copy-start | bytes 6148
  202.7 7.5 %copy-start.143 = (f32[1,512]{1,0:T(1,128)S(1)}, f32[1,512]{1,0:T(1,128)}, u32[]{:S(2)}) copy-start(f32[1,512]{1,0:T(1,128)} %get-tuple-element.159) | copy-start | bytes 6148
  202.8 9.2 %copy-start.159 = (f32[1,512]{1,0:T(1,128)S(1)}, f32[1,512]{1,0:T(1,128)}, u32[]{:S(2)}) copy-start(f32[1,512]{1,0:T(1,128)} %get-tuple-element.196) | copy-start | bytes 6148
  202.8 9.2 %copy-start.167 = (f32[1,512]{1,0:T(1,128)S(1)}, f32[1,512]{1,0:T(1,128)}, u32[]{:S(2)}) copy-start(f32[1,512]{1,0:T(1,128)} %get-tuple-element.197) | copy-start | bytes 6148
  202.8 9.2 %copy-start.172 = (f32[1,512]{1,0:T(1,128)S(1)}, f32[1,512]{1,0:T(1,128)}, u32[]{:S(2)}) copy-start(f32[1,512]{1,0:T(1,128)} %get-tuple-element.198) | copy-start | bytes 6148
  202.8 9.2 %copy-start.177 = (f32[1,512]{1,0:T(1,128)S(1)}, f32[1,512]{1,0:T(1,128)}, u32[]{:S(2)}) copy-start(f32[1,512]{1,0:T(1,128)} %get-tuple-element.199) | copy-start | bytes 6148
  202.8 9.2 %copy-start.182 = (f32[1,512]{1,0:T(1,128)S(1)}, f32[1,512]{1,0:T(1,128)}, u32[]{:S(2)}) copy-start(f32[1,512]{1,0:T(1,128)} %get-tuple-element.200) | copy-start | bytes 6148
  202.8 10.0 %copy-start.93 = (f32[1,512]{1,0:T(1,128)S(1)}, f32[1,512]{1,0:T(1,128)}, u32[]{:S(2)}) copy-start(f32[1,512]{1,0:T(1,128)} %get-tuple-element.187) | copy-start | bytes 6148
  202.8 10.0 %copy-start.103 = (f32[1,512]{1,0:T(1,128)S(1)}, f32[1,512]{1,0:T(1,128)}, u32[]{:S(2)}) copy-start(f32[1,512]{1,0:T(1,128)} %get-tuple-element.188) | copy-start | bytes 6148
  202.8 10.0 %copy-start.110 = (f32[1,512]{1,0:T(1,128)S(1)}, f32[1,512]{1,0:T(1,128)}, u32[]{:S(2)}) copy-start(f32[1,512]{1,0:T(1,128)} %get-tuple-element.190) | copy-start | bytes 6148
  202.8 10.0 %copy-start.116 = (f32[1,512]{1,0:T(1,128)S(1)}, f32[1,512]{1,0:T(1,128)}, u32[]{:S(2)}) copy-start(f32[1,512]{1,0:T(1,128)} %get-tuple-element.191) | copy-start | bytes 6148
  202.8 10.0 %copy-start.121 = (f32[1,512]{1,0:T(1,128)S(1)}, f32[1,512]{1,0:T(1,128)}, u32[]{:S(2)}) copy-start(f32[1,512]{1,0:T(1,128)} %get-tuple-element.192) | copy-start | bytes 6148
  202.9 10.0 %copy-start.127 = (f32[1,512]{1,0:T(1,128)S(1)}, f32[1,512]{1,0:T(1,128)}, u32[]{:S(2)}) copy-start(f32[1,512]{1,0:T(1,128)} %get-tuple-element.193) | copy-start | bytes 6148
  202.9 10.0 %copy-start.135 = (f32[1,512]{1,0:T(1,128)S(1)}, f32[1,512]{1,0:T(1,128)}, u32[]{:S(2)}) copy-start(f32[1,512]{1,0:T(1,128)} %get-tuple-element.194) | copy-start | bytes 6148
  202.9 10.0 %copy-start.141 = (f32[1,512]{1,0:T(1,128)S(1)}, f32[1,512]{1,0:T(1,128)}, u32[]{:S(2)}) copy-start(f32[1,512]{1,0:T(1,128)} %get-tuple-element.195) | copy-start | bytes 6148
  202.9 10.0 %copy-start.149 = (f32[1,512]{1,0:T(1,128)S(1)}, f32[1,512]{1,0:T(1,128)}, u32[]{:S(2)}) copy-start(f32[1,512]{1,0:T(1,128)} %get-tuple-element.189) | copy-start | bytes 6148
  202.9 10.1 %copy-start.12 = (f32[1,512]{1,0:T(1,128)S(1)}, f32[1,512]{1,0:T(1,128)}, u32[]{:S(2)}) copy-start(f32[1,512]{1,0:T(1,128)} %get-tuple-element.176) | copy-start | bytes 6148
  202.9 10.1 %copy-start.18 = (f32[1,512]{1,0:T(1,128)S(1)}, f32[1,512]{1,0:T(1,128)}, u32[]{:S(2)}) copy-start(f32[1,512]{1,0:T(1,128)} %get-tuple-element.177) | copy-start | bytes 6148
  202.9 10.1 %copy-start.25 = (f32[1,512]{1,0:T(1,128)S(1)}, f32[1,512]{1,0:T(1,128)}, u32[]{:S(2)}) copy-start(f32[1,512]{1,0:T(1,128)} %get-tuple-element.178) | copy-start | bytes 6148
  202.9 10.1 %copy-start.31 = (f32[1,512]{1,0:T(1,128)S(1)}, f32[1,512]{1,0:T(1,128)}, u32[]{:S(2)}) copy-start(f32[1,512]{1,0:T(1,128)} %get-tuple-element.179) | copy-start | bytes 6148
  202.9 10.1 %copy-start.37 = (f32[1,512]{1,0:T(1,128)S(1)}, f32[1,512]{1,0:T(1,128)}, u32[]{:S(2)}) copy-start(f32[1,512]{1,0:T(1,128)} %get-tuple-element.180) | copy-start | bytes 6148
  202.9 10.1 %copy-start.43 = (f32[1,512]{1,0:T(1,128)S(1)}, f32[1,512]{1,0:T(1,128)}, u32[]{:S(2)}) copy-start(f32[1,512]{1,0:T(1,128)} %get-tuple-element.181) | copy-start | bytes 6148
  203.0 10.1 %copy-start.49 = (f32[1,512]{1,0:T(1,128)S(1)}, f32[1,512]{1,0:T(1,128)}, u32[]{:S(2)}) copy-start(f32[1,512]{1,0:T(1,128)} %get-tuple-element.182) | copy-start | bytes 6148
  203.0 10.1 %copy-start.56 = (f32[1,512]{1,0:T(1,128)S(1)}, f32[1,512]{1,0:T(1,128)}, u32[]{:S(2)}) copy-start(f32[1,512]{1,0:T(1,128)} %get-tuple-element.183) | copy-start | bytes 6148
  203.0 10.1 %copy-start.63 = (f32[1,512]{1,0:T(1,128)S(1)}, f32[1,512]{1,0:T(1,128)}, u32[]{:S(2)}) copy-start(f32[1,512]{1,0:T(1,128)} %get-tuple-element.184) | copy-start | bytes 6148
  203.0 10.1 %copy-start.71 = (f32[1,512]{1,0:T(1,128)S(1)}, f32[1,512]{1,0:T(1,128)}, u32[]{:S(2)}) copy-start(f32[1,512]{1,0:T(1,128)} %get-tuple-element.185) | copy-start | bytes 6148
  203.0 10.1 %copy-start.82 = (f32[1,512]{1,0:T(1,128)S(1)}, f32[1,512]{1,0:T(1,128)}, u32[]{:S(2)}) copy-start(f32[1,512]{1,0:T(1,128)} %get-tuple-element.186) | copy-start | bytes 6148
  247.9 85.1 %copy-start.164 = (f32[1,512]{1,0:T(1,128)S(1)}, f32[1,512]{1,0:T(1,128)}, u32[]{:S(2)}) copy-start(f32[1,512]{1,0:T(1,128)} %get-tuple-element.162) | copy-start | bytes 6148
  247.9 85.1 %copy-start.201 = (f32[1,512]{1,0:T(1,128)S(1)}, f32[1,512]{1,0:T(1,128)}, u32[]{:S(2)}) copy-start(f32[1,512]{1,0:T(1,128)} %get-tuple-element.208) | copy-start | bytes 6148
  247.9 85.2 %copy-start.158 = (f32[1,512]{1,0:T(1,128)S(1)}, f32[1,512]{1,0:T(1,128)}, u32[]{:S(2)}) copy-start(f32[1,512]{1,0:T(1,128)} %get-tuple-element.161) | copy-start | bytes 6148
  247.9 85.2 %copy-start.199 = (f32[1,512]{1,0:T(1,128)S(1)}, f32[1,512]{1,0:T(1,128)}, u32[]{:S(2)}) copy-start(f32[1,512]{1,0:T(1,128)} %get-tuple-element.210) | copy-start | bytes 6148
  247.9 85.2 %copy-start.152 = (f32[1,512]{1,0:T(1,128)S(1)}, f32[1,512]{1,0:T(1,128)}, u32[]{:S(2)}) copy-start(f32[1,512]{1,0:T(1,128)} %get-tuple-element.160) | copy-start | bytes 6148
  247.9 85.2 %copy-start.198 = (f32[1,512]{1,0:T(1,128)S(1)}, f32[1,512]{1,0:T(1,128)}, u32[]{:S(2)}) copy-start(f32[1,512]{1,0:T(1,128)} %get-tuple-element.209) | copy-start | bytes 6148
  247.9 85.3 %copy-start.144 = (f32[1,512]{1,0:T(1,128)S(1)}, f32[1,512]{1,0:T(1,128)}, u32[]{:S(2)}) copy-start(f32[1,512]{1,0:T(1,128)} %get-tuple-element.159) | copy-start | bytes 6148
  248.0 85.3 %copy-start.202 = (f32[1,512]{1,0:T(1,128)S(1)}, f32[1,512]{1,0:T(1,128)}, u32[]{:S(2)}) copy-start(f32[1,512]{1,0:T(1,128)} %get-tuple-element.207) | copy-start | bytes 6148
  248.0 85.4 %copy-start.134 = (f32[1,512]{1,0:T(1,128)S(1)}, f32[1,512]{1,0:T(1,128)}, u32[]{:S(2)}) copy-start(f32[1,512]{1,0:T(1,128)} %get-tuple-element.158) | copy-start | bytes 6148
  248.0 85.4 %copy-start.200 = (f32[1,512]{1,0:T(1,128)S(1)}, f32[1,512]{1,0:T(1,128)}, u32[]{:S(2)}) copy-start(f32[1,512]{1,0:T(1,128)} %get-tuple-element.206) | copy-start | bytes 6148
  248.0 85.5 %copy-start.126 = (f32[1,512]{1,0:T(1,128)S(1)}, f32[1,512]{1,0:T(1,128)}, u32[]{:S(2)}) copy-start(f32[1,512]{1,0:T(1,128)} %get-tuple-element.157) | copy-start | bytes 6148
  248.0 85.5 %copy-start.197 = (f32[1,512]{1,0:T(1,128)S(1)}, f32[1,512]{1,0:T(1,128)}, u32[]{:S(2)}) copy-start(f32[1,512]{1,0:T(1,128)} %get-tuple-element.205) | copy-start | bytes 6148
  248.0 85.6 %copy-start.196 = (f32[1,512]{1,0:T(1,128)S(1)}, f32[1,512]{1,0:T(1,128)}, u32[]{:S(2)}) copy-start(f32[1,512]{1,0:T(1,128)} %get-tuple-element.204) | copy-start | bytes 6148
  258.5 75.2 %copy-start.193 = (f32[1,512]{1,0:T(1,128)S(1)}, f32[1,512]{1,0:T(1,128)}, u32[]{:S(2)}) copy-start(f32[1,512]{1,0:T(1,128)} %get-tuple-element.203) | copy-start | bytes 6148
  258.5 75.3 %copy-start.190 = (f32[1,512]{1,0:T(1,128)S(1)}, f32[1,512]{1,0:T(1,128)}, u32[]{:S(2)}) copy-start(f32[1,512]{1,0:T(1,128)} %get-tuple-element.202) | copy-start | bytes 6148
  258.5 75.4 %copy-start.187 = (f32[1,512]{1,0:T(1,128)S(1)}, f32[1,512]{1,0:T(1,128)}, u32[]{:S(2)}) copy-start(f32[1,512]{1,0:T(1,128)} %get-tuple-element.201) | copy-start | bytes 6148
  258.5 75.4 %copy-start.183 = (f32[1,512]{1,0:T(1,128)S(1)}, f32[1,512]{1,0:T(1,128)}, u32[]{:S(2)}) copy-start(f32[1,512]{1,0:T(1,128)} %get-tuple-element.200) | copy-start | bytes 6148
  258.6 75.5 %copy-start.178 = (f32[1,512]{1,0:T(1,128)S(1)}, f32[1,512]{1,0:T(1,128)}, u32[]{:S(2)}) copy-start(f32[1,512]{1,0:T(1,128)} %get-tuple-element.199) | copy-start | bytes 6148
  (149 other events, 261.9 us)
Sparse Core Ops, SparseCore 0:
  248.0 82.0 reduce-scatter.1
where the time goes:
time: 347 us; the launch traced here: 346 us
  waiting for transfers between devices  193 us (56%)
  local copies, waits for them, and re-layouts  35.9 us (10%)
  matrix products  34.4 us (10%)
  other arithmetic  26.4 us (8%)
  starting transfers between devices  19.5 us (6%)
  blocking collectives  19.2 us (6%)
  between operations  17.8 us (5%)
    all_to_all x1, waiting for transfers between devices, shards(): lax.all_to_all(picked.reshape(group_count, capacity, coef_count * local_c...  114 us
    reduce_scatter x1, waiting for transfers between devices, shards(): lax.psum_scatter(convolve(turned, weight_zero, weight_one, weight_two, mi...  71.5 us
    dot_general x9, matrix products, mixed_contract(): jnp.einsum(pattern, first_operand, second_operand, preferred_element_type...  14.5 us
    concatenate x1, local copies, waits for them, and re-layouts, convolve(): jnp.concatenate([out_zero, out_one_plus, out_one_minus, out_two_plus, out...  14.5 us
    all_to_all x1, starting transfers between devices, shards(): lax.all_to_all(requests, 'edge', split_axis=0, concat_axis=0, tiled=True)  13.6 us
    all_gather x1, blocking collectives, shards(): lax.all_gather(quarter.astype(jnp.bfloat16), 'chan', axis=0, tiled=True)  9.89 us
    all_gather x1, blocking collectives, shards(): lax.all_gather(quarter_fade.astype(jnp.bfloat16), 'chan', axis=0, tiled=T...  9.35 us
    convert_element_type x1, local copies, waits for them, and re-layouts, pick_rows(): jnp.dot(selector, table, preferred_element_type=jnp.float32)  9.26 us
  transfers between devices with their start and end apart: 3, of which 3 were waited for; matrix products, arithmetic and copies ran while one was open for 6% of the time, Pallas kernels for 0%

commit v1 on v0

--- a/solution.py
+++ b/solution.py
@@ -4,10 +4,13 @@
 import jax.numpy as jnp
 import numpy as np
 from jax import lax
+from jax.sharding import Mesh
 from jax.sharding import PartitionSpec as P
 
 LMAX = 6
 MMAX = 2
+EDGE_AXES = ("y", "z", "xl")
+CHAN_AXES = ("xh", "core")
 
 
 cutoff_radius = 6.0
@@ -131,22 +134,6 @@
     return jnp.stack(rows_out, axis=0).astype(jnp.bfloat16)
 
 
-def rotate_back(compact_t, scaled):
-    listing = row_offsets()
-    coefs_out = []
-    for degree in range(LMAX + 1):
-        for inner in range(2 * degree + 1):
-            total = None
-            for row_index, (row_degree, offset) in enumerate(listing):
-                if row_degree == degree:
-                    term = compact_t[offset + inner].astype(jnp.float32)[None, :] * scaled[
-                        :, row_index
-                    ].astype(jnp.float32)
-                    total = term if total is None else total + term
-            coefs_out.append(total)
-    return jnp.stack(coefs_out, axis=0).astype(jnp.bfloat16)
-
-
 def convolve(turned, weight_zero, weight_one, weight_two, contract):
     end_zero = LMAX + 1
     end_one_plus = end_zero + LMAX
@@ -157,7 +144,7 @@
     one_minus = turned[end_one_plus:end_one_minus]
     two_plus = turned[end_one_minus:end_two_plus]
     two_minus = turned[end_two_plus:]
-    pattern = "lce,lcjd->dje"
+    pattern = "lce,lcjd->jed"
     out_zero = contract(pattern, zero_part, weight_zero)
     out_one_plus = contract(pattern, one_plus, weight_one[0]) - contract(
         pattern, one_minus, weight_one[1]
@@ -172,7 +159,7 @@
         pattern, two_plus, weight_two[1]
     )
     return jnp.concatenate(
-        [out_zero, out_one_plus, out_one_minus, out_two_plus, out_two_minus], axis=1
+        [out_zero, out_one_plus, out_one_minus, out_two_plus, out_two_minus], axis=0
     )
 
 
@@ -182,17 +169,6 @@
 
 def one_hot(indices, width):
     return (indices[:, None] == jnp.arange(width, dtype=jnp.int32)[None, :]).astype(jnp.bfloat16)
-
-
-def pick_columns(table, selector):
-    picked = lax.dot_general(
-        table, selector, (((0,), (1,)), ((), ())), preferred_element_type=jnp.float32
-    )
-    return picked.astype(jnp.bfloat16)
-
-
-def pick_rows(selector, table):
-    return jnp.dot(selector, table, preferred_element_type=jnp.float32).astype(jnp.bfloat16)
 
 
 def shards(
@@ -210,72 +186,63 @@
     local_nodes = node_states.shape[0]
     local_channels = node_states.shape[2]
     coef_count = node_states.shape[1]
-    group_count = lax.axis_size("edge")
-    capacity = max(2, 2 * slab_size // group_count)
-    slot_total = group_count * capacity
-    quarter, quarter_fade = wigner_rows(edge_vectors)
-    compact, envelope = (
-        lax.all_gather(quarter.astype(jnp.bfloat16), "chan", axis=0, tiled=True),
-        lax.all_gather(quarter_fade.astype(jnp.bfloat16), "chan", axis=0, tiled=True),
-    )
-    compact_t = compact.T
+    group_count = lax.axis_size(EDGE_AXES)
     node_flat = node_states.reshape(local_nodes, coef_count * local_channels)
-    owner_part = source_part[:, 0]
-    owners = jnp.arange(group_count, dtype=jnp.int32)
-    member = (owner_part[:, None] == owners[None, :]).astype(jnp.int32)
-    earlier = jnp.cumsum(member, axis=0) - member
-    position = jnp.sum(earlier * member, axis=1)
-    slot_flat = owner_part * capacity + position
-    requests = (
-        jnp.zeros((slot_total,), jnp.int32)
-        .at[slot_flat]
-        .set(source_slot)
-        .reshape(group_count, capacity)
-    )
-    slot_select = one_hot(slot_flat, slot_total)
-    wanted = lax.all_to_all(requests, "edge", split_axis=0, concat_axis=0, tiled=True)
-    picked = pick_rows(one_hot(wanted.reshape(-1), local_nodes), node_flat)
-    returned = lax.all_to_all(
-        picked.reshape(group_count, capacity, coef_count * local_channels),
-        "edge",
-        split_axis=0,
-        concat_axis=0,
-        tiled=True,
-    )
-    sources = pick_columns(
-        returned.reshape(slot_total, coef_count * local_channels), slot_select
-    ).reshape(coef_count, local_channels, slab_size)
+    pair = lax.all_gather(node_flat, "xl", axis=0, tiled=True)
+    table = lax.all_gather(pair, ("y", "z"), axis=0, tiled=True)
+    vectors = lax.all_gather(edge_vectors, CHAN_AXES, axis=1, tiled=True)
+    compact, envelope = wigner_rows(vectors)
+    compact_t = compact.astype(jnp.bfloat16).T
+    source_index = source_part[:, 0] * local_nodes + source_slot
+    selector = one_hot(source_index, group_count * local_nodes)
+    sources = (
+        lax.dot_general(
+            table, selector, (((0,), (1,)), ((), ())), preferred_element_type=jnp.float32
+        )
+        .astype(jnp.bfloat16)
+        .reshape(coef_count, local_channels, slab_size)
+    )
     turned = rotate_forward(compact_t, sources)
-    channel_mix = lax.psum_scatter(
-        convolve(turned, weight_zero, weight_one, weight_two, mixed_contract).astype(jnp.bfloat16),
-        "chan",
-        scatter_dimension=0,
-        tiled=True,
-    ).astype(jnp.float32)
+    mixed = convolve(turned, weight_zero, weight_one, weight_two, mixed_contract).astype(
+        jnp.bfloat16
+    )
     alive_mask = (jnp.arange(slab_size, dtype=jnp.int32) < live_edges[0]).astype(jnp.float32)
-    scaling = envelope.astype(jnp.float32) * alive_mask
-    scaled = (channel_mix * scaling).astype(jnp.bfloat16)
-    message = rotate_back(compact_t, scaled).reshape(coef_count * local_channels, slab_size)
-    selector = (jnp.arange(local_nodes, dtype=jnp.int32)[:, None] == target_slot[None, :]).astype(
-        jnp.bfloat16
-    )
-    summed = lax.dot_general(
-        selector, message, (((1,), (1,)), ((), ())), preferred_element_type=jnp.float32
-    )
-    return summed.astype(jnp.bfloat16).reshape(local_nodes, coef_count, local_channels)
+    scaling = envelope * alive_mask
+    targets = jnp.where(
+        jnp.arange(local_nodes, dtype=jnp.int32)[:, None] == target_slot[None, :],
+        scaling[None, :],
+        0.0,
+    )
+    partial_out = []
+    listing = row_offsets()
+    for degree in range(LMAX + 1):
+        rows = [(r, o) for r, (d, o) in enumerate(listing) if d == degree]
+        left = jnp.stack(
+            [
+                targets[None, :, :] * compact_t[o : o + 2 * degree + 1].astype(jnp.float32)[:, None, :]
+                for _, o in rows
+            ]
+        ).astype(jnp.bfloat16)
+        right = jnp.stack([mixed[r] for r, _ in rows])
+        partial_out.append(
+            jnp.einsum("rkte,red->tkd", left, right, preferred_element_type=jnp.float32)
+        )
+    partial_sum = jnp.concatenate(partial_out, axis=1).astype(jnp.bfloat16)
+    return lax.psum_scatter(partial_sum, CHAN_AXES, scatter_dimension=2, tiled=True)
 
 
 def solution(mesh):
     in_specs = (
-        P("edge", None, "chan"),
-        P(None, ("edge", "chan")),
-        P("edge", None),
-        P("edge"),
-        P("edge"),
-        P("edge"),
-        P(None, "chan", None, None),
-        P(None, None, "chan", None, None),
-        P(None, None, "chan", None, None),
-    )
-    out_specs = P("edge", None, "chan")
-    return jax.shard_map(shards, mesh=mesh, in_specs=in_specs, out_specs=out_specs, check_vma=False)
+        P(EDGE_AXES, None, CHAN_AXES),
+        P(None, EDGE_AXES + CHAN_AXES),
+        P(EDGE_AXES, None),
+        P(EDGE_AXES),
+        P(EDGE_AXES),
+        P(EDGE_AXES),
+        P(None, CHAN_AXES, None, None),
+        P(None, None, CHAN_AXES, None, None),
+        P(None, None, CHAN_AXES, None, None),
+    )
+    out_specs = P(EDGE_AXES, None, CHAN_AXES)
+    fine = Mesh(mesh.devices.reshape(4, 8, 2, 2, 2), EDGE_AXES + CHAN_AXES)
+    return jax.shard_map(shards, mesh=fine, in_specs=in_specs, out_specs=out_specs, check_vma=False)

time: 347 us -> 191 us (0.55)
  waiting for transfers between devices: 193 us -> 82.7 us
  starting transfers between devices: 19.5 us -> 0.04 us
  other arithmetic: 26.4 us -> 15.9 us
  local copies, waits for them, and re-layouts: 35.9 us -> 27.9 us
  blocking collectives: 19.2 us -> 15.4 us
    all_to_all x2 -> x0, waiting for transfers between devices: 121 us -> none  [the longest x1 114 us: shards(): lax.all_to_all(picked.reshape(group_count, capacity, coef_count * local_c...]
    reduce_scatter x1 -> x0, waiting for transfers between devices: 71.5 us -> none  [shards(): lax.psum_scatter(convolve(turned, weight_zero, weight_one, weight_two, mi...]
    all_gather x0 -> x1, waiting for transfers between devices: none -> 51.9 us  [shards(): table = lax.all_gather(pair, ('y', 'z'), axis=0, tiled=True)]
    unnamed x1 -> x3, waiting for transfers between devices: 0.02 us -> 30.8 us
    unnamed x421 -> x281, local copies, waits for them, and re-layouts: 2.38 us -> 22.5 us
    all_to_all x2 -> x0, starting transfers between devices: 19.4 us -> none  [the longest x1 13.6 us: shards(): lax.all_to_all(requests, 'edge', split_axis=0, concat_axis=0, tiled=True)]
    concatenate x1 -> x0, local copies, waits for them, and re-layouts: 14.5 us -> none  [convolve(): jnp.concatenate([out_zero, out_one_plus, out_one_minus, out_two_plus, out...]
    convert_element_type x1 -> x0, local copies, waits for them, and re-layouts: 9.26 us -> none  [pick_rows(): jnp.dot(selector, table, preferred_element_type=jnp.float32)]
  transfers between devices with their start and end apart: 3 -> 2, of which waited for: 3 -> 2; matrix products, arithmetic and copies ran while one was open for 6% -> 15% of each run, Pallas kernels for 0% -> 0%
where the time goes in v1:
time: 191 us; the launch traced here: 190 us
  waiting for transfers between devices  82.7 us (43%)
  matrix products  32 us (17%)
  local copies, waits for them, and re-layouts  27.9 us (15%)
  between operations  16.4 us (9%)
  other arithmetic  15.9 us (8%)
  blocking collectives  15.4 us (8%)
    all_gather x1, waiting for transfers between devices, shards(): table = lax.all_gather(pair, ('y', 'z'), axis=0, tiled=True)  51.9 us
    unnamed x3, waiting for transfers between devices  30.8 us
    unnamed x281, local copies, waits for them, and re-layouts  22.5 us
    all_gather x1, blocking collectives, shards(): vectors = lax.all_gather(edge_vectors, CHAN_AXES, axis=1, tiled=True)  10.5 us
    dot_general x29, matrix products, wigner_rows(): pieces.append(jnp.dot(values[degree, azimuthal], table, precision=highest))  9.26 us
    dot_general x9, matrix products, mixed_contract(): jnp.einsum(pattern, first_operand, second_operand, preferred_element_type...  8.73 us
    dot_general x1, matrix products, shards(): lax.dot_general(table, selector, (((0,), (1,)), ((), ())), preferred_elem...  8.62 us
    unnamed x40, other arithmetic  8.32 us
  transfers between devices with their start and end apart: 2, of which 2 were waited for; matrix products, arithmetic and copies ran while one was open for 15% of the time, Pallas kernels for 0%

profile of v1, /device:TPU:1, one launch (start us, length us, event | category | flops | bytes accessed | tf_op | source)
XLA Modules:
  0.0 190.4 jit_solution(1929342396492727228)
XLA Ops:
  6.5 1.1 copy.51
  7.9 5.0 %all_gather.10 = bf16[32,3136]{1,0:T(8,128)(2,1)} all-gather(bf16[16,3136]{1,0:T(8,128)(2,1)S(1)} %reshape.2902), channel_id=1, replica_groups=mesh['y'=4,'z'=8,'xl'=2,'xh'=2,'core'=2] {'xl'}, dimensions={0}, use_global_device_ids=true | all-gather | bytes 301056 | tf_op jit(solution)/shard_map/all_gather | solution.py:191
  12.9 10.5 %all_gather.9 = f32[3,512]{1,0:T(4,128)S(1)} all-gather(f32[3,128]{1,0:T(4,128)} %param.42), channel_id=1, replica_groups=mesh['y'=4,'z'=8,'xl'=2,'xh'=2,'core'=2] {'xh','core'}, dimensions={1}, use_global_device_ids=true | all-gather | bytes 7680 | tf_op jit(solution)/shard_map/all_gather | solution.py:193
  24.3 0.7 fusion.512
  25.2 0.4 convolution_convert_fusion.1
  25.9 0.3 convolution_convert_fusion.2
  26.3 0.4 convolution_convert_fusion.4
  28.8 0.4 convolution_convert_fusion.7
  30.9 0.4 convolution_convert_fusion.13
  31.3 0.4 convolution_convert_fusion.14
  31.7 0.4 convolution_convert_fusion.15
  33.2 0.4 convolution_convert_fusion.8
  33.6 0.3 convolution_convert_fusion.9
  33.9 0.4 convolution_convert_fusion.10
  34.4 0.4 convolution_convert_fusion.11
  34.7 0.3 convolution_convert_fusion.12
  35.1 2.7 %concatenate.18 = bf16[512,235]{0,1:T(8,128)(2,1)S(1)} concatenate(bf16[512,1]{0,1:T(2,128)(2,1)S(1)} %dot_general.147, bf16[512,3]{0,1:T(4,128)(2,1)S(1)} %convolution_convert_fusion.29, bf16[512,5]{0,1:T(8,128)(2,1)S(1)} %convolution_convert_fusion.26, bf16[512,7]{0,1:T(8,128)(2,1)S(1)} %convolution_convert_fusion.25, bf16[512,9]{0,1:T(8,128)(2,1)S(1)} %convolution_convert_fusion.15, ...), dimensions={1} | concatenate | bytes 481280 | tf_op jit(solution)/shard_map/concatenate | solution.py:118
  37.9 0.7 slice_convert_fusion.51
  38.6 0.7 slice_convert_fusion.40
  39.2 0.6 slice_convert_fusion.105
  39.9 0.7 slice_convert_fusion.85
  40.6 0.7 slice_convert_fusion.178
  41.3 0.7 slice_convert_fusion.198
  41.9 0.6 slice_convert_fusion.176
  42.8 0.7 constant_dynamic-update-slice_fusion.38
  43.5 0.7 constant_dynamic-update-slice_fusion.37
  44.2 0.7 constant_dynamic-update-slice_fusion.36
  44.9 0.7 constant_dynamic-update-slice_fusion.35
  45.5 0.7 constant_dynamic-update-slice_fusion.34
  46.4 0.8 copy-done.11
  47.5 0.7 fusion.108
  48.2 0.8 fusion.109
  48.9 0.7 fusion.110
  49.7 0.7 fusion.111
  50.4 0.7 fusion.112
  51.1 1.3 fusion.663
  52.5 0.9 copy-done.1
  53.4 1.2 fusion.662
  54.6 51.9 %all-gather.2.cloned.1.call-done = bf16[1024,3136]{1,0:T(8,128)(2,1)} async-done(((bf16[32,3136]{1,0:T(8,128)(2,1)}), bf16[1024,3136]{1,0:T(8,128)(2,1)}) %all-gather.2.cloned.1.call-update) | async-done | bytes 6422544 | tf_op jit(solution)/shard_map/all_gather | solution.py:192
  106.5 8.6 %fusion = bf16[3136,512]{1,0:T(8,128)(2,1)S(1)} fusion(bf16[1024,3136]{1,0:T(8,128)(2,1)} %all-gather.2.cloned.1.call-done, s32[512]{0:T(512)S(1)} %add.1142), kind=kOutput, calls=%fused_computation.1 | convolution fusion | flops 3290464256 | bytes 9635840 | tf_op jit(solution)/shard_map/dot_general | solution.py:199
  116.2 1.1 fusion.5
  119.1 0.4 copy-done.6
  119.5 0.9 fusion.92
  121.5 0.9 fusion.93
  122.7 0.9 fusion.9
  123.7 0.9 fusion.8
  125.6 0.5 copy-done.3
  126.3 1.0 fusion.86
  128.4 1.0 fusion.87
  129.4 1.0 fusion.7
  130.4 1.0 fusion.6
  131.7 0.3 slice_dynamic-update-slice_fusion.1
  132.4 0.7 copy-done.14
  133.2 0.3 fusion.77
  133.5 1.5 fusion.71
  135.0 0.4 fusion.62
  135.4 0.8 copy-done.10
  136.2 0.4 fusion.50
  136.6 1.7 fusion.44
  138.3 6.8 %copy.72 = bf16[16,49,256]{0,1,2:T(8,128)(2,1)} copy(bf16[16,49,256]{2,0,1:T(8,128)(2,1)S(1)} %fusion.44) | data formatting | bytes 802816
  145.1 4.9 %reshape.3168 = bf16[256,784]{1,0:T(8,128)(2,1)} reshape(bf16[256,49,16]{2,1,0:T(8,128)(2,1)} %bitcast.836) | data formatting | bytes 802816
  150.1 30.8 %reduce-scatter.4.cloned.1.call-done = bf16[64,784]{1,0:T(8,128)(2,1)} async-done(((bf16[256,784]{1,0:T(8,128)(2,1)}), bf16[64,784]{1,0:T(8,128)(2,1)}) %reduce-scatter.4.cloned.1.call-update) | async-done | bytes 100368
  180.9 1.5 reshape.3169
  182.4 1.2 copy.73
  (368 shorter events, 12.2 us)
Async XLA Ops:
  6.5 109.6 %copy-start = (bf16[7,64,7,256]{3,1,2,0:T(8,128)(2,1)S(1)}, bf16[7,64,7,256]{3,1,2,0:T(8,128)(2,1)}, u32[]{:S(2)}) copy-start(bf16[7,64,7,256]{3,1,2,0:T(8,128)(2,1)} %param.47) | copy-start | bytes 4816900
  6.5 17.8 %copy-start.128 = (f32[3,98,1]{1,0,2:T(4,128)S(1)}, f32[3,98,1]{1,0,2:T(4,128)}, u32[]{:S(2)}) copy-start(f32[3,98,1]{1,0,2:T(4,128)} %constant.145) | copy-start | bytes 3532
  6.5 99.9 %all-gather.2.cloned.1.call-start = ((), (), s32[]{:S(2)}) async-start(), calls=%async_computation.1 | async-start | bytes 6758400 | tf_op jit(solution)/shard_map/all_gather | solution.py:192
  7.9 17.3 %copy-start.135 = (f32[98,13]{1,0:T(8,128)S(1)}, f32[98,13]{1,0:T(8,128)}, u32[]{:S(2)}) copy-start(f32[98,13]{1,0:T(8,128)} %constant.141.clone) | copy-start | bytes 15292
  12.9 168.0 %reduce-scatter.4.cloned.1.call-start = ((), (), s32[]{:S(2)}) async-start(), calls=%async_computation.2 | async-start | bytes 573440
  24.1 13.7 %copy-start.126 = (f32[512]{0:T(512)}, f32[512]{0:T(512)S(1)}, u32[]{:S(2)}) copy-start(f32[512]{0:T(512)S(1)} %get-tuple-element.325) | copy-start | bytes 6148
  31.7 1.2 copy-start.132
  31.7 1.3 copy-start.129
  34.3 3.5 %copy-start.130 = (s32[512]{0:T(512)S(1)}, s32[512]{0:T(512)}, u32[]{:S(2)}) copy-start(s32[512]{0:T(512)} %param.45) | copy-start | bytes 6148
  37.8 77.4 %copy-start.52 = (f32[1,512]{1,0:T(1,128)}, f32[1,512]{1,0:T(1,128)S(1)}, u32[]{:S(2)}) copy-start(f32[1,512]{1,0:T(1,128)S(1)} %get-tuple-element.313) | copy-start | bytes 6148
  42.8 2.8 %copy-start.13 = (bf16[5,5,16,512]{3,2,0,1:T(8,128)(2,1)}, bf16[5,5,16,512]{3,2,0,1:T(8,128)(2,1)S(1)}, u32[]{:S(2)}) copy-start(bf16[5,5,16,512]{3,2,0,1:T(8,128)(2,1)S(1)} %constant_dynamic-update-slice_fusion.29) | copy-start | bytes 1228804
  47.3 3.8 %copy-start.2 = (bf16[2,5,64,5,256]{4,2,3,1,0:T(8,128)(2,1)S(1)}, bf16[2,5,64,5,256]{4,2,3,1,0:T(8,128)(2,1)}, u32[]{:S(2)}) copy-start(bf16[2,5,64,5,256]{4,2,3,1,0:T(8,128)(2,1)} %param.49) | copy-start | bytes 4915204
  47.5 3.0 %copy-start.9 = (bf16[5,11,16,512]{3,2,0,1:T(8,128)(2,1)}, bf16[5,11,16,512]{3,2,0,1:T(8,128)(2,1)S(1)}, u32[]{:S(2)}) copy-start(bf16[5,11,16,512]{3,2,0,1:T(8,128)(2,1)S(1)} %fusion.181) | copy-start | bytes 2703364
  51.1 2.3 %copy-start.1 = (bf16[2,6,64,6,256]{4,2,3,1,0:T(8,128)(2,1)S(1)}, bf16[2,6,64,6,256]{4,2,3,1,0:T(8,128)(2,1)}, u32[]{:S(2)}) copy-start(bf16[2,6,64,6,256]{4,2,3,1,0:T(8,128)(2,1)} %param.48) | copy-start | bytes 7077892
  118.3 1.2 copy-start.6
  119.4 1.1 copy-start.83
  119.4 1.2 copy-start.84
  119.4 1.2 copy-start.85
  119.4 1.2 copy-start.86
  119.4 1.2 copy-start.87
  119.5 1.3 copy-start.66
  119.5 1.3 copy-start.67
  119.5 1.3 copy-start.119
  119.5 1.3 copy-start.120
  119.5 1.3 copy-start.121
  119.5 1.3 copy-start.122
  119.5 1.3 copy-start.123
  119.5 1.3 copy-start.124
  119.5 1.3 copy-start.125
  123.6 1.1 copy-start.63
  123.6 1.1 copy-start.64
  123.6 1.3 copy-start.54
  123.6 1.3 copy-start.55
  123.6 1.3 copy-start.56
  123.6 1.3 copy-start.57
  123.6 1.3 copy-start.58
  123.6 1.3 copy-start.59
  123.7 1.3 copy-start.60
  123.7 1.3 copy-start.61
  123.7 1.3 copy-start.62
  124.8 1.3 copy-start.3
  126.1 1.3 copy-start.47
  126.1 1.3 copy-start.48
  126.1 1.3 copy-start.49
  126.1 1.3 copy-start.50
  126.1 1.3 copy-start.51
  126.1 1.4 copy-start.33
  126.1 1.4 copy-start.34
  126.2 1.4 copy-start.35
  126.2 1.4 copy-start.36
  126.2 1.4 copy-start.37
  126.2 1.4 copy-start.38
  126.2 1.4 copy-start.39
  126.2 1.5 copy-start.24
  126.2 1.5 copy-start.25
  126.2 1.5 copy-start.26
  126.2 1.5 copy-start.27
  126.2 1.5 copy-start.28
  126.3 1.5 copy-start.29
  126.3 1.5 copy-start.30
  126.3 1.5 copy-start.31
  126.3 1.5 copy-start.32
  133.5 1.5 copy-start.12
  135.0 1.2 copy-start.10
  (74 other events, 61.0 us)
Sparse Core Ops, SparseCore 0:
  13.0 93.4 all-gather.1
  150.2 30.6 reduce-scatter.3

commit v2 on v1

v2 whole, which is shorter than its diff:
```python
import math

import jax
import jax.numpy as jnp
import numpy as np
from jax import lax
from jax.experimental import pallas as pl
from jax.experimental.pallas import tpu as pltpu
from jax.sharding import Mesh
from jax.sharding import PartitionSpec as P

LMAX = 6
MMAX = 2
EDGE_AXES = ("y", "z", "xl")
CHAN_AXES = ("xh", "core")
SIZE_Y, SIZE_Z, SIZE_XL, SIZE_XH, SIZE_CORE = 4, 8, 2, 2, 2
LANES = 128
COEFS = (LMAX + 1) ** 2

cutoff_radius = 6.0


def solid_harmonics(x, y, z, r2, degree_top, order_top):
    results = {}
    real_part = [x * 0.0 + 1.0]
    imag_part = [x * 0.0]
    for _ in range(order_top):
        new_real = x * real_part[-1] - y * imag_part[-1]
        new_imag = x * imag_part[-1] + y * real_part[-1]
        real_part.append(new_real)
        imag_part.append(new_imag)
    for m in range(order_top + 1):
        start = (-1.0) ** m * math.prod(range(2 * m - 1, 0, -2))
        legendre = {m: z * 0.0 + start}
        if m + 1 <= degree_top:
            legendre[m + 1] = z * ((2 * m + 1) * start)
        for l in range(m + 2, degree_top + 1):
            legendre[l] = z * legendre[l - 1] * ((2 * l - 1) / (l - m)) - r2 * legendre[l - 2] * (
                (l + m - 1) / (l - m)
            )
        for l in range(m, degree_top + 1):
            factor = harmonic_norm(l, m)
            if m == 0:
                results[l, 0] = factor * legendre[l]
            else:
                results[l, m] = math.sqrt(2.0) * factor * (legendre[l] * real_part[m])
                results[l, -m] = math.sqrt(2.0) * factor * (legendre[l] * imag_part[m])
    return results


def harmonic_norm(l, m):
    return math.sqrt(
        (2 * l + 1) / (4.0 * math.pi) * math.factorial(l - m) / math.factorial(l + m)
    )


def gradient_tables():
    count = 60
    steps = np.arange(count) + 0.5
    points = np.stack([np.cos(steps * 1.7), np.sin(steps * 2.3), np.cos(steps * 0.9 + 0.4)])
    base = solid_harmonics(*points, (points**2).sum(0), LMAX, LMAX)
    tables = {}
    for axis in range(3):
        moved = points.astype(np.complex128)
        moved[axis] += 1e-20j
        value = solid_harmonics(*moved, (moved**2).sum(0), LMAX, LMAX)
        for l in range(1, LMAX + 1):
            lower = np.stack([base[l - 1, m] for m in range(-l + 1, l)], axis=1)
            for m in range(-l, l + 1):
                fit = np.linalg.lstsq(lower, value[l, m].imag / 1e-20, rcond=None)[0]
                tables[l, axis, m] = [
                    (i - l + 1, float(g)) for i, g in enumerate(fit) if abs(g) > 1e-8
                ]
    return tables


def kept_rows():
    row_list = [(degree, 0) for degree in range(LMAX + 1)]
    for azimuthal in range(1, MMAX + 1):
        row_list += [(degree, azimuthal) for degree in range(azimuthal, LMAX + 1)]
        row_list += [(degree, -azimuthal) for degree in range(azimuthal, LMAX + 1)]
    return row_list


def row_offsets():
    listing = []
    offset = 0
    for degree, _ in kept_rows():
        listing.append((degree, offset))
        offset += 2 * degree + 1
    return listing


ROWS = kept_rows()
OFFSETS = row_offsets()
ROT_TOTAL = sum(2 * degree + 1 for degree, _ in ROWS)
DEGREE_ROWS = {
    degree: [i for i, (d, _) in enumerate(ROWS) if d == degree] for degree in range(LMAX + 1)
}
MIX_PLACE = {}
for _degree in range(LMAX + 1):
    for _row in DEGREE_ROWS[_degree]:
        MIX_PLACE[_row] = len(MIX_PLACE)
SECTIONS = ((0, 7, 0), (7, 6, 256), (13, 6, 512), (19, 5, 768), (24, 5, 1024))


def frame_kernel(place_ref, info_ref, rot_ref, edge_ref, index_ref):
    vx, vy, vz = info_ref[0], info_ref[1], info_ref[2]
    length = jnp.sqrt(vx * vx + vy * vy + vz * vz)
    ux, uy, uz = vx / length, vy / length, vz / length
    first = jnp.where(jnp.abs(ux) < 0.6, 1.0, 0.0)
    second = 1.0 - first
    ax, ay, az = -uz * second, uz * first, ux * second - uy * first
    norm = jnp.sqrt(ax * ax + ay * ay + az * az)
    ax, ay, az = ax / norm, ay / norm, az / norm
    bx, by, bz = uy * az - uz * ay, uz * ax - ux * az, ux * ay - uy * ax
    values = solid_harmonics(ux, uy, uz, 1.0, LMAX, LMAX)
    tables = gradient_tables()

    def along(direction, lower, l):
        products = {}
        out = {}
        for m in range(-l, l + 1):
            total = None
            for axis in range(3):
                for lower_m, g in tables[l, axis, m]:
                    if lower_m not in lower:
                        continue
                    key = (axis, lower_m)
                    if key not in products:
                        products[key] = direction[axis] * lower[lower_m]
                    term = products[key] * g
                    total = term if total is None else total + term
            out[m] = total
        return out

    a, b = (ax, ay, az), (bx, by, bz)
    grad_a, grad_b = {}, {}
    where = {(d, m): off for (d, m), (_, off) in zip(ROWS, OFFSETS)}

    def put(l, m, rows, factor):
        for i, k in enumerate(range(-l, l + 1)):
            rot_ref[where[l, m] + i] = rows[k] * factor

    for l in range(LMAX + 1):
        here = {m: values[l, m] for m in range(-l, l + 1)}
        put(l, 0, here, math.sqrt(4.0 * math.pi / (2 * l + 1)))
        if l >= 1:
            lower = {m: values[l - 1, m] for m in range(-l + 1, l)}
            grad_a[l] = along(a, lower, l)
            grad_b[l] = along(b, lower, l)
            k1 = math.sqrt(2.0) * harmonic_norm(l, 1) * (-l * (l + 1) / 2)
            put(l, 1, grad_a[l], 1.0 / k1)
            put(l, -1, grad_b[l], 1.0 / k1)
        if l >= 2:
            k2 = math.sqrt(2.0) * harmonic_norm(l, 2) * ((l + 2) * (l + 1) * l * (l - 1) / 8)
            aa = along(a, grad_a[l - 1], l)
            bb = along(b, grad_b[l - 1], l)
            ab = along(a, grad_b[l - 1], l)
            put(l, 2, {k: aa[k] - bb[k] for k in aa}, 1.0 / (4 * k2))
            put(l, -2, ab, 1.0 / (2 * k2))
    envelope = 0.5 * (jnp.cos(math.pi / cutoff_radius * length) + 1.0)
    edge_ref[0] = envelope * info_ref[5]
    edge_ref[1] = info_ref[4]
    source = info_ref[3].astype(jnp.int32)
    part = source >> 4
    far_y = (part >> 4) ^ place_ref[0]
    far_z = (place_ref[1] - ((part >> 1) & 7)) & 7
    far_x = (part & 1) ^ place_ref[2]
    index_ref[...] = (
        ((((far_y >> 1) * 8 + far_z) * 2 + (far_y & 1)) * 2 + far_x) * 16 + (source & 15)
    )


def edge_frames(info, place):
    return pl.pallas_call(
        frame_kernel,
        out_shape=(
            jax.ShapeDtypeStruct((ROT_TOTAL, 8, LANES), jnp.float32),
            jax.ShapeDtypeStruct((2, 8, LANES), jnp.float32),
            jax.ShapeDtypeStruct((8, LANES), jnp.int32),
        ),
        in_specs=[
            pl.BlockSpec(memory_space=pltpu.SMEM),
            pl.BlockSpec(memory_space=pltpu.VMEM),
        ],
        out_specs=(pl.BlockSpec(memory_space=pltpu.VMEM),) * 3,
        name="edge_frames",
    )(place, info)


def layer_kernel(
    rot_ref,
    edge_ref,
    index_ref,
    w0_ref,
    w1_ref,
    w2_ref,
    *rest,
    nodes,
    width,
    blocks,
):
    block_refs = rest[:blocks]
    out0_ref, out1_ref = rest[blocks : blocks + 2]
    table, hot, source, turned, mix, left, sems = rest[blocks + 2 :]
    rows = nodes // blocks
    copies = [
        pltpu.make_async_copy(
            block_refs[i], table.at[pl.ds(i * rows, rows)], sems.at[i]
        )
        for i in range(blocks)
    ]
    for copy in copies:
        copy.start()
    for g in range(8):
        number = lax.broadcasted_iota(jnp.int32, (nodes, LANES), 0)
        hot[:, g * LANES : (g + 1) * LANES] = jnp.where(
            number == index_ref[g : g + 1, :], 1.0, 0.0
        ).astype(jnp.bfloat16)
    for copy in copies:
        copy.wait()
    step = 4 * width
    total = COEFS * width
    for start in range(0, total, step):
        size = min(step, total - start)
        source[start : start + size, :] = lax.dot_general(
            table[:, start : start + size],
            hot[...],
            (((0,), (0,)), ((), ())),
            preferred_element_type=jnp.float32,
        )

    def turn(g, carry):
        lanes = pl.ds(pl.multiple_of(g * LANES, LANES), LANES)
        for first, count, base in SECTIONS:
            for n in range(count):
                degree, offset = OFFSETS[first + n]
                acc = None
                for k in range(2 * degree + 1):
                    at = (degree * degree + k) * width
                    term = rot_ref[offset + k, pl.ds(g, 1), :] * source[at : at + width, lanes]
                    acc = term if acc is None else acc + term
                turned[base + n * width : base + (n + 1) * width, lanes] = acc.astype(jnp.bfloat16)
        return carry

    lax.fori_loop(0, 8, turn, 0)

    half = 4 * LANES

    def slab(s, carry):
        cols = pl.ds(pl.multiple_of(s * half, half), half)

        def section(n):
            _, count, base = SECTIONS[n]
            return turned[base : base + count * width, cols]

        def apply(part, weight):
            return lax.dot_general(
                part, weight, (((0,), (0,)), ((), ())), preferred_element_type=jnp.float32
            )

        def keep(row, value):
            at = MIX_PLACE[row] * half
            mix[at : at + half, :] = value.astype(jnp.bfloat16)

        zero = section(0)
        for j in range(7):
            keep(j, apply(zero, w0_ref[:, j * 256 : (j + 1) * 256]))
        for weight, plus_at, minus_at in ((w1_ref, 1, 2), (w2_ref, 3, 4)):
            plus, minus = section(plus_at), section(minus_at)
            for j in range(SECTIONS[plus_at][1]):
                real = weight[0, :, j * 256 : (j + 1) * 256]
                imag = weight[1, :, j * 256 : (j + 1) * 256]
                keep(SECTIONS[plus_at][0] + j, apply(plus, real) - apply(minus, imag))
                keep(SECTIONS[minus_at][0] + j, apply(minus, real) + apply(plus, imag))
        slots = lax.broadcasted_iota(jnp.int32, (16, LANES), 0).astype(jnp.float32)
        masks = [
            jnp.where(
                slots == edge_ref[1, pl.ds(s * 4 + g, 1), :],
                edge_ref[0, pl.ds(s * 4 + g, 1), :],
                0.0,
            )
            for g in range(4)
        ]
        for degree in range(LMAX + 1):
            members = DEGREE_ROWS[degree]
            for place, row in enumerate(members):
                offset = OFFSETS[row][1]
                for k in range(2 * degree + 1):
                    for g in range(4):
                        at = place * half + g * LANES
                        left[k * 16 : (k + 1) * 16, at : at + LANES] = (
                            masks[g] * rot_ref[offset + k, pl.ds(s * 4 + g, 1), :]
                        ).astype(jnp.bfloat16)
            depth = len(members) * half
            first = MIX_PLACE[members[0]] * half
            height = (2 * degree + 1) * 16
            result = jnp.dot(
                left[:height, :depth],
                mix[first : first + depth, :],
                preferred_element_type=jnp.float32,
            )
            at = pl.ds(pl.multiple_of(s * (COEFS * 16) + degree * degree * 16, 16), height)
            out0_ref[at, :] = jnp.concatenate(
                [result[:, 0:64], result[:, 128:192]], axis=1
            ).astype(jnp.bfloat16)
            out1_ref[at, :] = jnp.concatenate(
                [result[:, 64:128], result[:, 192:256]], axis=1
            ).astype(jnp.bfloat16)
        return carry

    lax.fori_loop(0, 2, slab, 0)


def layer(rot, edge, index, w0, w1, w2, block_list):
    blocks = len(block_list)
    rows, features = block_list[0].shape
    nodes = blocks * rows
    width = features // COEFS
    vmem = pl.BlockSpec(memory_space=pltpu.VMEM)

    def body(*refs):
        layer_kernel(*refs, nodes=nodes, width=width, blocks=blocks)

    shape = jax.ShapeDtypeStruct((2 * COEFS * 16, LANES), jnp.bfloat16)
    return pl.pallas_call(
        body,
        out_shape=(shape, shape),
        in_specs=[vmem] * 6 + [pl.BlockSpec(memory_space=pl.ANY)] * blocks,
        out_specs=(vmem, vmem),
        scratch_shapes=[
            pltpu.VMEM((nodes, features), jnp.bfloat16),
            pltpu.VMEM((nodes, 8 * LANES), jnp.bfloat16),
            pltpu.VMEM((features, 8 * LANES), jnp.float32),
            pltpu.VMEM((1280, 8 * LANES), jnp.bfloat16),
            pltpu.VMEM((len(ROWS) * 4 * LANES, 256), jnp.bfloat16),
            pltpu.VMEM((208, 5 * 4 * LANES), jnp.bfloat16),
            pltpu.SemaphoreType.DMA((blocks,)),
        ],
        compiler_params=pltpu.CompilerParams(vmem_limit_bytes=60 * 1024 * 1024),
        name="layer",
    )(rot, edge, index, w0, w1, w2, *block_list)


def move(block, flip_y=0, shift_z=0, flip_x=0):
    pairs = []
    for y in range(SIZE_Y):
        for z in range(SIZE_Z):
            for x in range(SIZE_XL):
                pairs.append(
                    (
                        (y * SIZE_Z + z) * SIZE_XL + x,
                        ((y ^ flip_y) * SIZE_Z + (z + shift_z) % SIZE_Z) * SIZE_XL + (x ^ flip_x),
                    )
                )
    return lax.ppermute(block, EDGE_AXES, pairs)


def gather_blocks(own, other):
    near = jnp.concatenate(
        [own, move(other, flip_x=1), move(own, flip_y=1), move(other, flip_y=1, flip_x=1)], axis=0
    )
    far = move(near, flip_y=2)
    first, second = {0: near}, {0: far}
    for s in range(1, 4):
        for ring in (first, second):
            ring[s] = move(ring[s - 1], shift_z=1)
            ring[8 - s] = move(ring[(9 - s) % 8], shift_z=-1)
    first[4] = move(first[3], shift_z=1)
    second[4] = move(second[5], shift_z=-1)
    return [first[s] for s in range(8)] + [second[s] for s in range(8)]


def shards(
    node_states,
    edge_vectors,
    source_part,
    source_slot,
    target_slot,
    live_edges,
    weight_zero,
    weight_one,
    weight_two,
):
    local_nodes, coef_count, local_channels = node_states.shape
    half_channels = local_channels // 2
    quarter = edge_vectors.shape[1]
    at_y, at_z, at_x = lax.axis_index("y"), lax.axis_index("z"), lax.axis_index("xl")
    at_h, at_c = lax.axis_index("xh"), lax.axis_index("core")
    begin = (at_h * SIZE_CORE + at_c) * quarter

    def mine(array):
        return lax.dynamic_slice_in_dim(array, begin, quarter, 0)

    source = mine(source_part[:, 0]) * local_nodes + mine(source_slot)
    alive = (begin + jnp.arange(quarter, dtype=jnp.int32)) < live_edges[0]
    info = jnp.concatenate(
        [
            edge_vectors,
            jnp.stack(
                [
                    source.astype(jnp.float32),
                    mine(target_slot).astype(jnp.float32),
                    alive.astype(jnp.float32),
                ]
            ),
        ],
        axis=0,
    )
    info = lax.all_gather(info, ("xl", "xh", "core"), axis=1)
    place = jnp.stack([at_y, at_z, at_x]).astype(jnp.int32)
    rot, edge, index = edge_frames(info, place)

    halves = node_states.reshape(local_nodes, coef_count, 2, half_channels)
    own = lax.dynamic_index_in_dim(halves, at_x, 2, keepdims=False)
    other = lax.dynamic_index_in_dim(halves, 1 - at_x, 2, keepdims=False)
    features = coef_count * half_channels
    block_list = gather_blocks(
        own.reshape(local_nodes, features), other.reshape(local_nodes, features)
    )

    low = at_x * half_channels
    w0 = lax.dynamic_slice_in_dim(weight_zero, low, half_channels, 1).reshape(
        7 * half_channels, 7 * 256
    )
    w1 = lax.dynamic_slice_in_dim(weight_one, low, half_channels, 2).reshape(
        2, 6 * half_channels, 6 * 256
    )
    w2 = lax.dynamic_slice_in_dim(weight_two, low, half_channels, 2).reshape(
        2, 5 * half_channels, 5 * 256
    )
    part0, part1 = layer(rot, edge, index, w0, w1, w2, block_list)

    swap = [(0, 1), (1, 0)]
    kept = jnp.where(at_c == 0, part0, part1)
    sent = jnp.where(at_c == 0, part1, part0)
    summed = kept.astype(jnp.float32) + lax.ppermute(sent, "core", swap).astype(jnp.float32)
    rows = coef_count * local_nodes
    summed = summed.reshape(2, rows, LANES)
    to_send = lax.dynamic_index_in_dim(summed, 1 - at_x, 0, keepdims=False).astype(jnp.bfloat16)
    summed = lax.dynamic_index_in_dim(summed, at_x, 0, keepdims=False)
    summed = summed + lax.ppermute(to_send, "xl", swap).astype(jnp.float32)

    def packed(value):
        return jnp.concatenate([value[: rows // 2], value[rows // 2 :]], axis=1)

    low_part, high_part = packed(summed[:, :64]), packed(summed[:, 64:])
    to_send = jnp.where(at_h == 0, high_part, low_part).astype(jnp.bfloat16)
    stay = jnp.where(at_h == 0, low_part, high_part)
    stay = stay + lax.ppermute(to_send, "xh", swap).astype(jnp.float32)
    stay = stay.astype(jnp.bfloat16)
    stay = jnp.concatenate([stay[:, :64], stay[:, 64:]], axis=0)
    return stay.reshape(coef_count, local_nodes, local_channels).transpose(1, 0, 2)


def solution(mesh):
    in_specs = (
        P(EDGE_AXES, None, CHAN_AXES),
        P(None, EDGE_AXES + CHAN_AXES),
        P(EDGE_AXES, None),
        P(EDGE_AXES),
        P(EDGE_AXES),
        P(EDGE_AXES),
        P(None, CHAN_AXES, None, None),
        P(None, None, CHAN_AXES, None, None),
        P(None, None, CHAN_AXES, None, None),
    )
    out_specs = P(EDGE_AXES, None, CHAN_AXES)
    fine = Mesh(
        mesh.devices.reshape(SIZE_Y, SIZE_Z, SIZE_XL, SIZE_XH, SIZE_CORE), EDGE_AXES + CHAN_AXES
    )
    return jax.shard_map(
        shards, mesh=fine, in_specs=in_specs, out_specs=out_specs, check_vma=False
    )
```

time: 191 us -> 123 us (0.64)
  waiting for transfers between devices: 82.7 us -> 17.1 us
  starting transfers between devices: 0.04 us -> 33.6 us
  matrix products: 32 us -> 0 us
  Pallas kernels: 0 us -> 26.3 us
  between operations: 16.4 us -> 0.87 us
  other arithmetic: 15.9 us -> 4.7 us
  local copies, waits for them, and re-layouts: 27.9 us -> 19 us
  blocking collectives: 15.4 us -> 20.1 us
    all_gather x1 -> x0, waiting for transfers between devices: 51.9 us -> none  [shards(): table = lax.all_gather(pair, ('y', 'z'), axis=0, tiled=True)]
    ppermute x0 -> x21, starting transfers between devices: none -> 33.6 us  [the longest x18 29.6 us: move(): return lax.ppermute(block, EDGE_AXES, pairs)]
    dot_general x47 -> x0, matrix products: 32 us -> none  [the longest x29 9.26 us: wigner_rows(): pieces.append(jnp.dot(values[degree, azimuthal], table, precision=highest))]
    unnamed x3 -> x0, waiting for transfers between devices: 30.8 us -> none
    pallas_call x0 -> x2, Pallas kernels: none -> 26.3 us  [the longest x1 24.2 us: layer(): pl.pallas_call(body, out_shape=(shape, shape), in_specs=[vmem] * 6 + [pl....]
    unnamed x281 -> x20, local copies, waits for them, and re-layouts: 22.5 us -> 4 us
    ppermute x0 -> x21, waiting for transfers between devices: none -> 17.1 us  [the longest x18 6.9 us: move(): return lax.ppermute(block, EDGE_AXES, pairs)]
    unnamed x40 -> x0, other arithmetic: 8.32 us -> none
  transfers between devices with their start and end apart: 2 -> 21, of which waited for: 2 -> 7; matrix products, arithmetic and copies ran while one was open for 15% -> 14% of each run, Pallas kernels for 0% -> 2%
where the time goes in v2:
time: 123 us; the launch traced here: 122 us
  starting transfers between devices  33.6 us (27%)
  Pallas kernels  26.3 us (21%)
  blocking collectives  20.1 us (16%)
  local copies, waits for them, and re-layouts  19 us (15%)
  waiting for transfers between devices  17.1 us (14%)
  other arithmetic  4.7 us (4%)
    ppermute x18, starting transfers between devices, move(): return lax.ppermute(block, EDGE_AXES, pairs)  29.6 us
    pallas_call x1, Pallas kernels, layer(): pl.pallas_call(body, out_shape=(shape, shape), in_specs=[vmem] * 6 + [pl....  24.2 us
    all_gather x1, blocking collectives, shards(): info = lax.all_gather(info, ('xl', 'xh', 'core'), axis=1)  20.1 us
    ppermute x18, waiting for transfers between devices, move(): return lax.ppermute(block, EDGE_AXES, pairs)  6.9 us
    ppermute x1, waiting for transfers between devices, shards(): summed = summed + lax.ppermute(to_send, 'xl', swap).astype(jnp.float32)  6.08 us
    unnamed x20, local copies, waits for them, and re-layouts  4 us
    reshape x1, local copies, waits for them, and re-layouts, shards(): lax.dynamic_slice_in_dim(weight_one, low, half_channels, 2)  3.76 us
    dynamic_slice x2, local copies, waits for them, and re-layouts, shards(): lax.dynamic_slice_in_dim(weight_two, low, half_channels, 2)  2.88 us
  transfers between devices with their start and end apart: 21, of which 7 were waited for; matrix products, arithmetic and copies ran while one was open for 14% of the time, Pallas kernels for 2%

profile of v2, /device:TPU:1, one launch (start us, length us, event | category | flops | bytes accessed | tf_op | source)
XLA Modules:
  0.0 121.6 jit_solution(16047101992490455488)
XLA Ops:
  0.0 1.3 %copy.18 = bf16[16,49,64]{1,2,0:T(8,128)(2,1)S(1)} copy(bf16[16,49,64]{2,0,1:T(8,128)(2,1)} %param.9) | data formatting | bytes 200704 | tf_op args[0]
  1.4 0.0 copy-start.6
  1.4 0.2 copy.20
  1.6 0.2 reshape.48
  1.8 2.1 %collective-permute-start = (bf16[16,1568]{1,0:T(8,128)(2,1)S(1)}, bf16[16,1568]{1,0:T(8,128)(2,1)S(1)}, u32[]{:S(2)}, u32[]{:S(2)}) collective-permute-start(bf16[16,1568]{1,0:T(8,128)(2,1)S(1)} %reshape.48), channel_id=1, source_target_pairs={{0,4},{4,0},{8,12},{12,8},{16,20},{20,16},{24,28},{28,24},{32,36},... | collective-permute-start | bytes 150536 | tf_op jit(solution)/shard_map/ppermute | solution.py:357
  3.9 1.3 %collective-permute-start.2 = (bf16[16,1568]{1,0:T(8,128)(2,1)S(1)}, bf16[16,1568]{1,0:T(8,128)(2,1)S(1)}, u32[]{:S(2)}, u32[]{:S(2)}) collective-permute-start(bf16[16,1568]{1,0:T(8,128)(2,1)S(1)} %reshape.48), channel_id=1, source_target_pairs={{0,68},{4,64},{8,76},{12,72},{16,84},{20,80},{24,92},{28,88},{32,1... | collective-permute-start | bytes 150536 | tf_op jit(solution)/shard_map/ppermute | solution.py:357
  5.1 0.2 copy.19
  5.3 0.2 reshape.47
  5.5 0.1 collective-permute-start.1
  5.7 3.1 %collective-permute-done.1 = bf16[16,1568]{1,0:T(8,128)(2,1)S(1)} collective-permute-done((bf16[16,1568]{1,0:T(8,128)(2,1)S(1)}, bf16[16,1568]{1,0:T(8,128)(2,1)S(1)}, u32[]{:S(2)}, u32[]{:S(2)}) %collective-permute-start.1) | collective-permute-done | bytes 50208 | tf_op jit(solution)/shard_map/ppermute | solution.py:357
  8.8 2.8 %collective-permute-start.10 = (bf16[64,1568]{1,0:T(8,128)(2,1)S(1)}, bf16[64,1568]{1,0:T(8,128)(2,1)}, u32[]{:S(2)}, u32[]{:S(2)}) collective-permute-start(bf16[64,1568]{1,0:T(8,128)(2,1)S(1)} %constant_dynamic-update-slice_fusion.refs_6_), channel_id=1, source_target_pairs={{0,128},{4,132},{8,136},{12,140},{16,144},{20,148},{24,152},{28,15... | collective-permute-start | bytes 602120 | tf_op jit(solution)/shard_map/ppermute | solution.py:357
  11.6 1.6 %collective-permute-start.3 = (bf16[64,1568]{1,0:T(8,128)(2,1)S(1)}, bf16[64,1568]{1,0:T(8,128)(2,1)}, u32[]{:S(2)}, u32[]{:S(2)}) collective-permute-start(bf16[64,1568]{1,0:T(8,128)(2,1)S(1)} %constant_dynamic-update-slice_fusion.refs_6_), channel_id=1, source_target_pairs={{0,8},{4,12},{8,16},{12,20},{16,24},{20,28},{24,32},{28,36},{32,40... | collective-permute-start | bytes 602120 | tf_op jit(solution)/shard_map/ppermute | solution.py:357
  13.3 1.9 %collective-permute-done.10.refs_14_ = bf16[64,1568]{1,0:T(8,128)(2,1)} collective-permute-done((bf16[64,1568]{1,0:T(8,128)(2,1)S(1)}, bf16[64,1568]{1,0:T(8,128)(2,1)}, u32[]{:S(2)}, u32[]{:S(2)}) %collective-permute-start.10) | collective-permute-done | bytes 200736 | tf_op jit(solution)/shard_map/ppermute | solution.py:357
  15.2 6.9 %collective-permute-start.14 = (bf16[64,1568]{1,0:T(8,128)(2,1)}, bf16[64,1568]{1,0:T(8,128)(2,1)}, u32[]{:S(2)}, u32[]{:S(2)}) collective-permute-start(bf16[64,1568]{1,0:T(8,128)(2,1)} %collective-permute-done.10.refs_14_), channel_id=1, source_target_pairs={{0,56},{4,60},{8,0},{12,4},{16,8},{20,12},{24,16},{28,20},{32,24},... | collective-permute-start | bytes 602120 | tf_op jit(solution)/shard_map/ppermute | solution.py:357
  22.7 0.8 convert_bitcast_fusion
  23.5 0.7 collective-permute-start.7
  24.3 0.7 collective-permute-start.11
  25.0 0.0 collective-permute-done.3.refs_7_
  25.0 0.0 collective-permute-start.4
  25.0 0.2 collective-permute-done.14.refs_21_
  25.2 3.1 %collective-permute-start.15 = (bf16[64,1568]{1,0:T(8,128)(2,1)}, bf16[64,1568]{1,0:T(8,128)(2,1)}, u32[]{:S(2)}, u32[]{:S(2)}) collective-permute-start(bf16[64,1568]{1,0:T(8,128)(2,1)} %collective-permute-done.14.refs_21_), channel_id=1, source_target_pairs={{0,56},{4,60},{8,0},{12,4},{16,8},{20,12},{24,16},{28,20},{32,24},... | collective-permute-start | bytes 602120 | tf_op jit(solution)/shard_map/ppermute | solution.py:357
  28.3 1.2 constant_dynamic-slice_fusion.4
  29.5 0.0 collective-permute-done.7.refs_13_
  29.5 3.1 %collective-permute-start.8 = (bf16[64,1568]{1,0:T(8,128)(2,1)}, bf16[64,1568]{1,0:T(8,128)(2,1)}, u32[]{:S(2)}, u32[]{:S(2)}) collective-permute-start(bf16[64,1568]{1,0:T(8,128)(2,1)} %collective-permute-done.7.refs_13_), channel_id=1, source_target_pairs={{0,56},{4,60},{8,0},{12,4},{16,8},{20,12},{24,16},{28,20},{32,24},... | collective-permute-start | bytes 602120 | tf_op jit(solution)/shard_map/ppermute | solution.py:357
  32.6 1.6 %collective-permute-done.4.refs_8_ = bf16[64,1568]{1,0:T(8,128)(2,1)} collective-permute-done((bf16[64,1568]{1,0:T(8,128)(2,1)}, bf16[64,1568]{1,0:T(8,128)(2,1)}, u32[]{:S(2)}, u32[]{:S(2)}) %collective-permute-start.4) | collective-permute-done | bytes 200736 | tf_op jit(solution)/shard_map/ppermute | solution.py:357
  34.3 0.0 collective-permute-start.5
  34.3 0.0 collective-permute-done.15.refs_20_
  34.3 2.9 %collective-permute-start.16 = (bf16[64,1568]{1,0:T(8,128)(2,1)}, bf16[64,1568]{1,0:T(8,128)(2,1)}, u32[]{:S(2)}, u32[]{:S(2)}) collective-permute-start(bf16[64,1568]{1,0:T(8,128)(2,1)} %collective-permute-done.15.refs_20_), channel_id=1, source_target_pairs={{0,56},{4,60},{8,0},{12,4},{16,8},{20,12},{24,16},{28,20},{32,24},... | collective-permute-start | bytes 602120 | tf_op jit(solution)/shard_map/ppermute | solution.py:357
  37.2 20.1 %all-gather = f32[6,1024]{1,0:T(8,128)S(1)} all-gather(f32[6,128]{1,0:T(8,128)S(1)} %pad_maximum_fusion.3), channel_id=2, replica_groups=mesh['y'=4,'z'=8,'xl'=2,'xh'=2,'core'=2] {'xl','xh','core'}, dimensions={1}, use_global_device_ids=true | all-gather | bytes 27648 | tf_op jit(solution)/shard_map/all_gather | solution.py:411
  57.3 0.6 copy.24
  57.9 0.5 copy.15
  58.4 1.1 copy.22
  59.5 0.1 constant_dynamic-slice_fusion.3
  59.7 2.0 %copy.16 = bf16[2,6,32,6,256]{4,3,2,1,0:T(8,128)(2,1)} copy(bf16[2,6,32,6,256]{4,2,3,1,0:T(8,128)(2,1)S(1)} %constant_dynamic-slice_fusion.3) | data formatting | bytes 2359296 | tf_op jit(solution)/shard_map/dynamic_slice | solution.py:427
  61.6 3.8 %reshape.44.refs_4_ = bf16[2,192,1536]{2,1,0:T(8,128)(2,1)} reshape(bf16[2,6,32,6,256]{4,3,2,1,0:T(8,128)(2,1)} %copy.16) | data formatting | bytes 2359296 | tf_op jit(solution)/shard_map/reshape | solution.py:427
  65.4 0.1 collective-permute-start.9
  65.5 1.4 %collective-permute-start.6 = (bf16[64,1568]{1,0:T(8,128)(2,1)}, bf16[64,1568]{1,0:T(8,128)(2,1)S(1)}, u32[]{:S(2)}, u32[]{:S(2)}) collective-permute-start(bf16[64,1568]{1,0:T(8,128)(2,1)} %collective-permute-done.5.refs_9_), channel_id=1, source_target_pairs={{0,8},{4,12},{8,16},{12,20},{16,24},{20,28},{24,32},{28,36},{32,40... | collective-permute-start | bytes 602120 | tf_op jit(solution)/shard_map/ppermute | solution.py:357
  66.9 0.0 collective-permute-done.12.refs_16_
  66.9 0.1 collective-permute-start.13
  67.0 2.6 %collective-permute-start.17 = (bf16[64,1568]{1,0:T(8,128)(2,1)}, bf16[64,1568]{1,0:T(8,128)(2,1)S(1)}, u32[]{:S(2)}, u32[]{:S(2)}) collective-permute-start(bf16[64,1568]{1,0:T(8,128)(2,1)} %collective-permute-done.16.refs_19_), channel_id=1, source_target_pairs={{0,56},{4,60},{8,0},{12,4},{16,8},{20,12},{24,16},{28,20},{32,24},... | collective-permute-start | bytes 602120 | tf_op jit(solution)/shard_map/ppermute | solution.py:357
  69.6 1.2 constant_dynamic-slice_fusion.2
  70.8 1.7 %copy.17 = bf16[2,5,32,5,256]{4,3,2,1,0:T(8,128)(2,1)} copy(bf16[2,5,32,5,256]{4,2,3,1,0:T(8,128)(2,1)S(1)} %constant_dynamic-slice_fusion.2) | data formatting | bytes 1638400 | tf_op jit(solution)/shard_map/dynamic_slice | solution.py:430
  72.4 2.8 %reshape.45.refs_5_ = bf16[2,160,1280]{2,1,0:T(8,128)(2,1)} reshape(bf16[2,5,32,5,256]{4,3,2,1,0:T(8,128)(2,1)} %copy.17) | data formatting | bytes 1638400 | tf_op jit(solution)/shard_map/reshape | solution.py:430
  75.2 0.6 pad_add_fusion.place_ref
  75.9 2.1 %edge_frames.1 = (f32[235,8,128]{2,1,0:T(8,128)}, f32[2,8,128]{2,1,0:T(8,128)}, s32[8,128]{1,0:T(8,128)}) custom-call(s32[3]{0:T(128)} %pad_add_fusion.place_ref, f32[6,8,128]{2,1,0:T(8,128)} %bitcast.41), custom_call_target="tpu_custom_call" | custom-call | tf_op jit(solution)/shard_map/edge_frames/pallas_call | solution.py:176
  78.1 0.6 copy-done.2
  78.7 0.1 copy-done.3
  78.8 0.1 copy-done.4
  78.8 0.1 copy-done.5
  79.0 24.2 %layer.1 = (bf16[1568,128]{1,0:T(8,128)(2,1)}, bf16[1568,128]{1,0:T(8,128)(2,1)}) custom-call(f32[235,8,128]{2,1,0:T(8,128)} %get-tuple-element.10.refs_0_, f32[2,8,128]{2,1,0:T(8,128)} %get-tuple-element.11.refs_1_, s32[8,128]{1,0:T(8,128)} %get-tuple-element.12.refs_2_, bf16[224,1792]{1,0:T(8,128)(2,1)} %bitcast.36, ...), custom_call_target="tpu_custom_call" | custom-call | tf_op jit(solution)/shard_map/layer/pallas_call | solution.py:327
  103.2 1.1 broadcast_select_fusion
  104.2 1.4 %collective-permute-start.18 = (bf16[1568,128]{1,0:T(8,128)(2,1)S(1)}, bf16[1568,128]{1,0:T(8,128)(2,1)S(1)}, u32[]{:S(2)}, u32[]{:S(2)}) collective-permute-start(bf16[1568,128]{1,0:T(8,128)(2,1)S(1)} %broadcast_select_fusion), channel_id=1, source_target_pairs={{0,1},{1,0},{2,3},{3,2},{4,5},{5,4},{6,7},{7,6},{8,9},{9,8},{10,11... | collective-permute-start | bytes 1204232 | tf_op jit(solution)/shard_map/ppermute | solution.py:438
  105.6 1.4 %collective-permute-done.18 = bf16[1568,128]{1,0:T(8,128)(2,1)S(1)} collective-permute-done((bf16[1568,128]{1,0:T(8,128)(2,1)S(1)}, bf16[1568,128]{1,0:T(8,128)(2,1)S(1)}, u32[]{:S(2)}, u32[]{:S(2)}) %collective-permute-start.18) | collective-permute-done | bytes 401440 | tf_op jit(solution)/shard_map/ppermute | solution.py:438
  107.0 1.1 convert_add_fusion
  108.1 0.7 fusion
  108.8 0.3 collective-permute-start.19
  109.1 6.1 %collective-permute-done.19 = bf16[784,128]{1,0:T(8,128)(2,1)S(1)} collective-permute-done((bf16[784,128]{1,0:T(8,128)(2,1)}, bf16[784,128]{1,0:T(8,128)(2,1)S(1)}, u32[]{:S(2)}, u32[]{:S(2)}) %collective-permute-start.19) | collective-permute-done | bytes 200736 | tf_op jit(solution)/shard_map/ppermute | solution.py:443
  115.2 0.2 fusion.4
  115.4 0.1 select_convert_fusion
  115.5 2.4 %collective-permute-start.20 = (bf16[392,128]{1,0:T(8,128)(2,1)S(1)}, bf16[392,128]{1,0:T(8,128)(2,1)S(1)}, u32[]{:S(2)}, u32[]{:S(2)}) collective-permute-start(bf16[392,128]{1,0:T(8,128)(2,1)S(1)} %select_convert_fusion), channel_id=1, source_target_pairs={{0,2},{2,0},{1,3},{3,1},{4,6},{6,4},{5,7},{7,5},{8,10},{10,8},{9,1... | collective-permute-start | bytes 301064 | tf_op jit(solution)/shard_map/ppermute | solution.py:451
  117.9 2.7 %collective-permute-done.20 = bf16[392,128]{1,0:T(8,128)(2,1)S(1)} collective-permute-done((bf16[392,128]{1,0:T(8,128)(2,1)S(1)}, bf16[392,128]{1,0:T(8,128)(2,1)S(1)}, u32[]{:S(2)}, u32[]{:S(2)}) %collective-permute-start.20) | collective-permute-done | bytes 100384 | tf_op jit(solution)/shard_map/ppermute | solution.py:451
  120.6 0.2 add_convert_fusion
  120.8 0.1 fusion.5
  120.9 0.7 pad_maximum_fusion.2
  (28 shorter events, 0.2 us)
Async XLA Ops:
  0.0 59.5 %copy-start = (bf16[2,6,64,6,256]{4,2,3,1,0:T(8,128)(2,1)S(1)}, bf16[2,6,64,6,256]{4,2,3,1,0:T(8,128)(2,1)}, u32[]{:S(2)}) copy-start(bf16[2,6,64,6,256]{4,2,3,1,0:T(8,128)(2,1)} %param.16) | copy-start | bytes 7077892
  1.4 35.8 %copy-start.6 = (f32[3,128]{1,0:T(4,128)S(1)}, f32[3,128]{1,0:T(4,128)}, u32[]{:S(2)}) copy-start(f32[3,128]{1,0:T(4,128)} %param.10) | copy-start | bytes 4612
  1.8 3.9 %collective-permute-start = (bf16[16,1568]{1,0:T(8,128)(2,1)S(1)}, bf16[16,1568]{1,0:T(8,128)(2,1)S(1)}, u32[]{:S(2)}, u32[]{:S(2)}) collective-permute-start(bf16[16,1568]{1,0:T(8,128)(2,1)S(1)} %reshape.48), channel_id=1, source_target_pairs={{0,4},{4,0},{8,12},{12,8},{16,20},{20,16},{24,28},{28,24},{32,36},... | collective-permute-start | bytes 150536 | tf_op jit(solution)/shard_map/ppermute | solution.py:357
  3.9 4.9 %collective-permute-start.2 = (bf16[16,1568]{1,0:T(8,128)(2,1)S(1)}, bf16[16,1568]{1,0:T(8,128)(2,1)S(1)}, u32[]{:S(2)}, u32[]{:S(2)}) collective-permute-start(bf16[16,1568]{1,0:T(8,128)(2,1)S(1)} %reshape.48), channel_id=1, source_target_pairs={{0,68},{4,64},{8,76},{12,72},{16,84},{20,80},{24,92},{28,88},{32,1... | collective-permute-start | bytes 150536 | tf_op jit(solution)/shard_map/ppermute | solution.py:357
  5.5 3.3 %collective-permute-start.1 = (bf16[16,1568]{1,0:T(8,128)(2,1)S(1)}, bf16[16,1568]{1,0:T(8,128)(2,1)S(1)}, u32[]{:S(2)}, u32[]{:S(2)}) collective-permute-start(bf16[16,1568]{1,0:T(8,128)(2,1)S(1)} %reshape.47), channel_id=1, source_target_pairs={{0,64},{4,68},{8,72},{12,76},{16,80},{20,84},{24,88},{28,92},{32,9... | collective-permute-start | bytes 150536 | tf_op jit(solution)/shard_map/ppermute | solution.py:357
  8.8 49.6 %copy-start.1 = (bf16[64,1568]{1,0:T(8,128)(2,1)}, bf16[64,1568]{1,0:T(8,128)(2,1)S(1)}, u32[]{:S(2)}) copy-start(bf16[64,1568]{1,0:T(8,128)(2,1)S(1)} %constant_dynamic-update-slice_fusion.refs_6_) | copy-start | bytes 602116
  8.8 6.4 %collective-permute-start.10 = (bf16[64,1568]{1,0:T(8,128)(2,1)S(1)}, bf16[64,1568]{1,0:T(8,128)(2,1)}, u32[]{:S(2)}, u32[]{:S(2)}) collective-permute-start(bf16[64,1568]{1,0:T(8,128)(2,1)S(1)} %constant_dynamic-update-slice_fusion.refs_6_), channel_id=1, source_target_pairs={{0,128},{4,132},{8,136},{12,140},{16,144},{20,148},{24,152},{28,15... | collective-permute-start | bytes 602120 | tf_op jit(solution)/shard_map/ppermute | solution.py:357
  11.6 13.4 %collective-permute-start.3 = (bf16[64,1568]{1,0:T(8,128)(2,1)S(1)}, bf16[64,1568]{1,0:T(8,128)(2,1)}, u32[]{:S(2)}, u32[]{:S(2)}) collective-permute-start(bf16[64,1568]{1,0:T(8,128)(2,1)S(1)} %constant_dynamic-update-slice_fusion.refs_6_), channel_id=1, source_target_pairs={{0,8},{4,12},{8,16},{12,20},{16,24},{20,28},{24,32},{28,36},{32,40... | collective-permute-start | bytes 602120 | tf_op jit(solution)/shard_map/ppermute | solution.py:357
  15.2 10.0 %collective-permute-start.14 = (bf16[64,1568]{1,0:T(8,128)(2,1)}, bf16[64,1568]{1,0:T(8,128)(2,1)}, u32[]{:S(2)}, u32[]{:S(2)}) collective-permute-start(bf16[64,1568]{1,0:T(8,128)(2,1)} %collective-permute-done.10.refs_14_), channel_id=1, source_target_pairs={{0,56},{4,60},{8,0},{12,4},{16,8},{20,12},{24,16},{28,20},{32,24},... | collective-permute-start | bytes 602120 | tf_op jit(solution)/shard_map/ppermute | solution.py:357
  23.5 6.0 %collective-permute-start.7 = (bf16[64,1568]{1,0:T(8,128)(2,1)S(1)}, bf16[64,1568]{1,0:T(8,128)(2,1)}, u32[]{:S(2)}, u32[]{:S(2)}) collective-permute-start(bf16[64,1568]{1,0:T(8,128)(2,1)S(1)} %constant_dynamic-update-slice_fusion.refs_6_), channel_id=1, source_target_pairs={{0,56},{4,60},{8,0},{12,4},{16,8},{20,12},{24,16},{28,20},{32,24},... | collective-permute-start | bytes 602120 | tf_op jit(solution)/shard_map/ppermute | solution.py:357
  24.3 10.0 %collective-permute-start.11 = (bf16[64,1568]{1,0:T(8,128)(2,1)}, bf16[64,1568]{1,0:T(8,128)(2,1)}, u32[]{:S(2)}, u32[]{:S(2)}) collective-permute-start(bf16[64,1568]{1,0:T(8,128)(2,1)} %collective-permute-done.10.refs_14_), channel_id=1, source_target_pairs={{0,8},{4,12},{8,16},{12,20},{16,24},{20,28},{24,32},{28,36},{32,40... | collective-permute-start | bytes 602120 | tf_op jit(solution)/shard_map/ppermute | solution.py:357
  25.0 9.2 %collective-permute-start.4 = (bf16[64,1568]{1,0:T(8,128)(2,1)}, bf16[64,1568]{1,0:T(8,128)(2,1)}, u32[]{:S(2)}, u32[]{:S(2)}) collective-permute-start(bf16[64,1568]{1,0:T(8,128)(2,1)} %collective-permute-done.3.refs_7_), channel_id=1, source_target_pairs={{0,8},{4,12},{8,16},{12,20},{16,24},{20,28},{24,32},{28,36},{32,40... | collective-permute-start | bytes 602120 | tf_op jit(solution)/shard_map/ppermute | solution.py:357
  25.2 9.1 %collective-permute-start.15 = (bf16[64,1568]{1,0:T(8,128)(2,1)}, bf16[64,1568]{1,0:T(8,128)(2,1)}, u32[]{:S(2)}, u32[]{:S(2)}) collective-permute-start(bf16[64,1568]{1,0:T(8,128)(2,1)} %collective-permute-done.14.refs_21_), channel_id=1, source_target_pairs={{0,56},{4,60},{8,0},{12,4},{16,8},{20,12},{24,16},{28,20},{32,24},... | collective-permute-start | bytes 602120 | tf_op jit(solution)/shard_map/ppermute | solution.py:357
  29.5 35.9 %collective-permute-start.8 = (bf16[64,1568]{1,0:T(8,128)(2,1)}, bf16[64,1568]{1,0:T(8,128)(2,1)}, u32[]{:S(2)}, u32[]{:S(2)}) collective-permute-start(bf16[64,1568]{1,0:T(8,128)(2,1)} %collective-permute-done.7.refs_13_), channel_id=1, source_target_pairs={{0,56},{4,60},{8,0},{12,4},{16,8},{20,12},{24,16},{28,20},{32,24},... | collective-permute-start | bytes 602120 | tf_op jit(solution)/shard_map/ppermute | solution.py:357
  34.3 31.3 %collective-permute-start.5 = (bf16[64,1568]{1,0:T(8,128)(2,1)}, bf16[64,1568]{1,0:T(8,128)(2,1)}, u32[]{:S(2)}, u32[]{:S(2)}) collective-permute-start(bf16[64,1568]{1,0:T(8,128)(2,1)} %collective-permute-done.4.refs_8_), channel_id=1, source_target_pairs={{0,8},{4,12},{8,16},{12,20},{16,24},{20,28},{24,32},{28,36},{32,40... | collective-permute-start | bytes 602120 | tf_op jit(solution)/shard_map/ppermute | solution.py:357
  34.3 32.6 %collective-permute-start.12 = (bf16[64,1568]{1,0:T(8,128)(2,1)}, bf16[64,1568]{1,0:T(8,128)(2,1)}, u32[]{:S(2)}, u32[]{:S(2)}) collective-permute-start(bf16[64,1568]{1,0:T(8,128)(2,1)} %collective-permute-done.11.refs_15_), channel_id=1, source_target_pairs={{0,8},{4,12},{8,16},{12,20},{16,24},{20,28},{24,32},{28,36},{32,40... | collective-permute-start | bytes 602120 | tf_op jit(solution)/shard_map/ppermute | solution.py:357
  34.3 32.7 %collective-permute-start.16 = (bf16[64,1568]{1,0:T(8,128)(2,1)}, bf16[64,1568]{1,0:T(8,128)(2,1)}, u32[]{:S(2)}, u32[]{:S(2)}) collective-permute-start(bf16[64,1568]{1,0:T(8,128)(2,1)} %collective-permute-done.15.refs_20_), channel_id=1, source_target_pairs={{0,56},{4,60},{8,0},{12,4},{16,8},{20,12},{24,16},{28,20},{32,24},... | collective-permute-start | bytes 602120 | tf_op jit(solution)/shard_map/ppermute | solution.py:357
  65.4 12.6 %collective-permute-start.9 = (bf16[64,1568]{1,0:T(8,128)(2,1)}, bf16[64,1568]{1,0:T(8,128)(2,1)S(1)}, u32[]{:S(2)}, u32[]{:S(2)}) collective-permute-start(bf16[64,1568]{1,0:T(8,128)(2,1)} %collective-permute-done.8.refs_12_), channel_id=1, source_target_pairs={{0,56},{4,60},{8,0},{12,4},{16,8},{20,12},{24,16},{28,20},{32,24},... | collective-permute-start | bytes 602120 | tf_op jit(solution)/shard_map/ppermute | solution.py:357
  65.5 12.5 %collective-permute-start.6 = (bf16[64,1568]{1,0:T(8,128)(2,1)}, bf16[64,1568]{1,0:T(8,128)(2,1)S(1)}, u32[]{:S(2)}, u32[]{:S(2)}) collective-permute-start(bf16[64,1568]{1,0:T(8,128)(2,1)} %collective-permute-done.5.refs_9_), channel_id=1, source_target_pairs={{0,8},{4,12},{8,16},{12,20},{16,24},{20,28},{24,32},{28,36},{32,40... | collective-permute-start | bytes 602120 | tf_op jit(solution)/shard_map/ppermute | solution.py:357
  66.9 11.1 %collective-permute-start.13 = (bf16[64,1568]{1,0:T(8,128)(2,1)}, bf16[64,1568]{1,0:T(8,128)(2,1)S(1)}, u32[]{:S(2)}, u32[]{:S(2)}) collective-permute-start(bf16[64,1568]{1,0:T(8,128)(2,1)} %collective-permute-done.12.refs_16_), channel_id=1, source_target_pairs={{0,8},{4,12},{8,16},{12,20},{16,24},{20,28},{24,32},{28,36},{32,40... | collective-permute-start | bytes 602120 | tf_op jit(solution)/shard_map/ppermute | solution.py:357
  67.0 11.1 %collective-permute-start.17 = (bf16[64,1568]{1,0:T(8,128)(2,1)}, bf16[64,1568]{1,0:T(8,128)(2,1)S(1)}, u32[]{:S(2)}, u32[]{:S(2)}) collective-permute-start(bf16[64,1568]{1,0:T(8,128)(2,1)} %collective-permute-done.16.refs_19_), channel_id=1, source_target_pairs={{0,56},{4,60},{8,0},{12,4},{16,8},{20,12},{24,16},{28,20},{32,24},... | collective-permute-start | bytes 602120 | tf_op jit(solution)/shard_map/ppermute | solution.py:357
  78.0 0.7 copy-start.2
  78.0 0.8 copy-start.3
  78.0 0.8 copy-start.4
  78.1 0.9 copy-start.5
  104.2 2.7 %collective-permute-start.18 = (bf16[1568,128]{1,0:T(8,128)(2,1)S(1)}, bf16[1568,128]{1,0:T(8,128)(2,1)S(1)}, u32[]{:S(2)}, u32[]{:S(2)}) collective-permute-start(bf16[1568,128]{1,0:T(8,128)(2,1)S(1)} %broadcast_select_fusion), channel_id=1, source_target_pairs={{0,1},{1,0},{2,3},{3,2},{4,5},{5,4},{6,7},{7,6},{8,9},{9,8},{10,11... | collective-permute-start | bytes 1204232 | tf_op jit(solution)/shard_map/ppermute | solution.py:438
  108.8 6.4 %collective-permute-start.19 = (bf16[784,128]{1,0:T(8,128)(2,1)}, bf16[784,128]{1,0:T(8,128)(2,1)S(1)}, u32[]{:S(2)}, u32[]{:S(2)}) collective-permute-start(bf16[784,128]{1,0:T(8,128)(2,1)} %fusion), channel_id=1, source_target_pairs={{0,4},{4,0},{1,5},{5,1},{2,6},{6,2},{3,7},{7,3},{8,12},{12,8},{9,1... | collective-permute-start | bytes 602120 | tf_op jit(solution)/shard_map/ppermute | solution.py:443
  115.5 5.1 %collective-permute-start.20 = (bf16[392,128]{1,0:T(8,128)(2,1)S(1)}, bf16[392,128]{1,0:T(8,128)(2,1)S(1)}, u32[]{:S(2)}, u32[]{:S(2)}) collective-permute-start(bf16[392,128]{1,0:T(8,128)(2,1)S(1)} %select_convert_fusion), channel_id=1, source_target_pairs={{0,2},{2,0},{1,3},{3,1},{4,6},{6,4},{5,7},{7,5},{8,10},{10,8},{9,1... | collective-permute-start | bytes 301064 | tf_op jit(solution)/shard_map/ppermute | solution.py:451
